TPU v7x, 32 devices: a whole 2x2x4 slice. The times are simulated.
32 devices in a mesh: grp: 8 (over z, x), ep: 4 (over y, core).
Axes of the slice: x: 2, y: 2, z: 4, core: 2. Of those that a mesh axis runs over, the one named last changes fastest.
Arguments:
- out_grad: bfloat16 [256, 4096], P('grp', 'ep'), may hold values from -6 to 6
- expert_ids: int32 [256, 8], P('grp'), may hold values from 0 to 15, as said below
- router_logits: float32 [256, 16], P('grp'), may hold values from -5 to 5
- router_weight: bfloat16 [16, 4096], P(None, 'ep'), may hold values from -0.09375 to 0.09375
- expert_weight: bfloat16 [16, 4096, 1024], P('grp', 'ep'), may hold values from -0.1875 to 0.1875
- hidden_saved: bfloat16 [8, 512, 1024], P('grp'), may hold values from -6 to 6
Outputs:
- weight_grad: bfloat16 [16, 4096, 1024], P('grp', 'ep')
- hidden_grad: bfloat16 [8, 512, 1024], P('grp', 'ep')
- input_grad: bfloat16 [256, 4096], P('grp', 'ep')
Inputs may be any that keep to these rules, and one draw needn't show every extreme that they name: `expert_ids`: each row names 8 different experts, lying in at most 4 of the 4 groups of 4 consecutive experts. In each aligned block of 32 rows no expert is named by more than 32 rows, and some expert is named by exactly 32.
All inputs are finite; a program needn't handle non-finite values.
Results may differ from a plain program's by a relative error of at most 0.02.
Values may be sent and summed in bfloat16 or wider, within the bound.
A program may use at most 64 MiB of HBM per device.

v0:
```python
import jax
import jax.numpy as jnp
from jax import lax
from jax.experimental import pallas as pl
from jax.experimental.pallas import tpu as pltpu
from jax.sharding import PartitionSpec as P

route_scale = 2.5


def body(out_grad, expert_ids, router_logits, router_weight, expert_weight, hidden_saved):
    group_rows, features = out_grad.shape
    top_count = expert_ids.shape[1]
    experts = router_logits.shape[1]
    group_count = lax.axis_size("grp")
    local_experts = expert_weight.shape[0]
    hidden_width = expert_weight.shape[2]
    slot_count = hidden_saved.shape[1]
    capacity = slot_count // (local_experts * group_count)
    expert_span = group_count * capacity
    pair_count = group_rows * top_count
    sig_values = jax.nn.sigmoid(router_logits)
    picked = expert_ids[:, :, None] == jnp.arange(experts, dtype=jnp.int32)[None, None, :]
    chosen = jnp.sum(jnp.where(picked, sig_values[:, None, :], 0.0), axis=2)
    route_probs = route_scale * chosen / jnp.sum(chosen, axis=1, keepdims=True)
    flat_ids = expert_ids.reshape(pair_count)
    onehot = picked.reshape(pair_count, experts).astype(jnp.int32)
    pair_ranks = jnp.sum((jnp.cumsum(onehot, axis=0) - 1) * onehot, axis=1)
    slot_place = (
        flat_ids % local_experts * group_count + flat_ids // local_experts
    ) * capacity + pair_ranks
    slot_match = slot_place[None, :] == jnp.arange(slot_count, dtype=jnp.int32)[:, None]
    token_pick = jnp.sum(
        slot_match.reshape(slot_count, group_rows, top_count).astype(jnp.float32), axis=2
    ).astype(jnp.bfloat16)
    send_rows = jnp.dot(token_pick, out_grad, preferred_element_type=jnp.float32).astype(
        jnp.bfloat16
    )
    send_prob = jnp.sum(
        jnp.where(slot_match, route_probs.reshape(1, pair_count), 0.0), axis=1
    ).astype(jnp.bfloat16)
    got_rows, got_prob = (
        lax.all_to_all(
            send_rows.reshape(local_experts, group_count, capacity, features),
            "grp",
            split_axis=1,
            concat_axis=1,
            tiled=True,
        ),
        lax.all_to_all(
            send_prob.reshape(local_experts, group_count, capacity),
            "grp",
            split_axis=1,
            concat_axis=1,
            tiled=True,
        ),
    )
    slot_grads = got_rows.reshape(local_experts, expert_span, features)
    prob_rows = got_prob.reshape(local_experts, expert_span).astype(jnp.float32)
    saved_rows = hidden_saved.reshape(local_experts, expert_span, hidden_width)
    scaled_rows = (prob_rows[:, :, None] * slot_grads.astype(jnp.float32)).astype(jnp.bfloat16)
    weight_grad = jnp.einsum(
        "lmd,lmf->ldf", scaled_rows, saved_rows, preferred_element_type=jnp.float32
    ).astype(jnp.bfloat16)
    owner_index = lax.axis_index("ep")
    share_rows = slot_count // lax.axis_size("ep")
    flat_prob = prob_rows.reshape(slot_count)
    flat_saved = hidden_saved.reshape(slot_count, hidden_width)
    partial_term = jnp.einsum(
        "lmd,ldf->lmf", slot_grads, expert_weight, preferred_element_type=jnp.float32
    ).reshape(slot_count, hidden_width)
    rounded_term = lax.optimization_barrier(partial_term.astype(jnp.bfloat16)).astype(jnp.float32)
    partial_score = jnp.sum(flat_saved.astype(jnp.float32) * rounded_term, axis=1)
    moved_scores = lax.all_to_all(
        partial_score.reshape(local_experts, group_count, capacity),
        "grp",
        split_axis=1,
        concat_axis=1,
        tiled=True,
    )
    returned = lax.psum(moved_scores, "ep")
    summed = lax.psum_scatter(
        partial_term.astype(jnp.bfloat16), "ep", scatter_dimension=0, tiled=True
    ).astype(jnp.float32)
    own_prob = lax.dynamic_slice_in_dim(flat_prob, owner_index * share_rows, share_rows, 0)
    hidden_grad = (own_prob[:, None] * summed).astype(jnp.bfloat16)[None]
    pair_score = jnp.sum(
        jnp.where(slot_match, returned.reshape(slot_count, 1), 0.0), axis=0
    ).reshape(group_rows, top_count)
    weighted_mean = jnp.sum(route_probs * pair_score, axis=1, keepdims=True) / route_scale
    logit_terms = route_probs * (1.0 - chosen) * (pair_score - weighted_mean)
    router_grad = jnp.sum(jnp.where(picked, logit_terms[:, :, None], 0.0), axis=1).astype(
        jnp.bfloat16
    )
    input_grad = jnp.dot(router_grad, router_weight, preferred_element_type=jnp.float32).astype(
        jnp.bfloat16
    )
    return (weight_grad, hidden_grad, input_grad)


MESH = pl.DeviceIdType.MESH


def fused_kernel(
    ids_ref, logits_ref, grad_ref, rw_ref, w_hbm, saved_hbm,
    scaled_ref, hidden_ref, input_ref,
    w_ref, saved_ref, rows_all, probs_all, probs_own, slot_ref, slot_rows, prob_col, part,
    recv_a, send_b, recv_b, score_own, score_recv, score_rows,
    w_sem, saved_sem, rows_send, rows_recv, probs_send, probs_recv,
    a_send, a_recv, b_send, b_recv, sc_send, sc_recv,
):
    groups = lax.axis_size("grp")
    parts = lax.axis_size("ep")
    chips = parts // 2
    g = lax.axis_index("grp")
    k = lax.axis_index("ep")
    chip, core = k // 2, k % 2
    rows, features = grad_ref.shape
    experts = logits_ref.shape[0]
    top = ids_ref.shape[0]
    local, span, width = part.shape
    half_groups = groups // 2
    half_tokens = half_groups * rows
    tokens = groups * rows
    share = span // 2
    capacity = span // groups
    f32, bf16 = jnp.float32, jnp.bfloat16

    barrier = pltpu.get_barrier_semaphore()
    for dg in range(groups):
        for dk in range(parts):
            if dg or dk:
                pl.semaphore_signal(
                    barrier, inc=1,
                    device_id=(lax.rem(g + dg, groups), lax.rem(k + dk, parts)),
                    device_id_type=MESH,
                )
    w_copies = [
        pltpu.make_async_copy(w_hbm.at[i], w_ref.at[i], w_sem.at[i]) for i in range(local)
    ]
    for copy in w_copies:
        copy.start()
    saved_copy = pltpu.make_async_copy(saved_hbm, saved_ref, saved_sem)
    saved_copy.start()

    sig = 1.0 / (1.0 + jnp.exp(-logits_ref[...]))
    ids = ids_ref[...]
    expert_iota = lax.broadcasted_iota(jnp.int32, (experts, rows), 0)
    named = ids[0:1, :] == expert_iota
    for i in range(1, top):
        named = named | (ids[i : i + 1, :] == expert_iota)
    probs = route_scale * sig / jnp.sum(jnp.where(named, sig, 0.0), axis=0, keepdims=True)
    probs = jnp.where(named, probs, 0.0)
    lane_off = lax.rem(g, half_groups) * rows
    place = (
        lax.broadcasted_iota(jnp.int32, (rows, half_tokens), 1)
        == lax.broadcasted_iota(jnp.int32, (rows, half_tokens), 0) + lane_off
    )
    placed = jnp.dot(
        probs.astype(bf16), place.astype(f32).astype(bf16), preferred_element_type=f32
    ).astype(bf16)
    probs_own[...] = placed
    probs_all[g] = placed
    rows_all[pl.ds(pl.multiple_of(g * rows, rows), rows), :] = grad_ref[...]

    pl.semaphore_wait(barrier, groups * parts - 1)

    parity, pos = lax.rem(g, 2), g // 2
    mate = g + 1 - 2 * parity

    def block(b):
        return rows_all.at[pl.ds(pl.multiple_of(b * rows, rows), rows), :]

    def rows_copy(src, b, to, sem):
        return pltpu.make_async_remote_copy(
            src_ref=src, dst_ref=block(b), send_sem=rows_send.at[sem], recv_sem=rows_recv.at[b],
            device_id=(to, k), device_id_type=MESH,
        )

    sends = []
    peers = [lax.rem(pos + j, half_groups) * 2 + parity for j in range(1, half_groups)]
    for j in range(1, groups):
        to = lax.rem(g + j, groups)
        copy = pltpu.make_async_remote_copy(
            src_ref=probs_own, dst_ref=probs_all.at[g],
            send_sem=probs_send.at[j - 1], recv_sem=probs_recv.at[g],
            device_id=(to, k), device_id_type=MESH,
        )
        copy.start()
        sends.append(copy)
    for n, to in enumerate([*peers, mate]):
        copy = rows_copy(grad_ref, g, to, n)
        copy.start()
        sends.append(copy)
    for n, peer in enumerate(peers):
        rows_copy(block(peer), peer, g, 0).wait_recv()
        copy = rows_copy(block(peer), peer, mate, half_groups + n)
        copy.start()
        sends.append(copy)

    for j in range(1, groups):
        b = lax.rem(g + j, groups)
        pltpu.make_async_remote_copy(
            src_ref=probs_own, dst_ref=probs_all.at[b],
            send_sem=probs_send.at[0], recv_sem=probs_recv.at[b],
            device_id=(g, k), device_id_type=MESH,
        ).wait_recv()
    pick = (
        lax.broadcasted_iota(jnp.int32, (8, experts), 1)
        == lax.broadcasted_iota(jnp.int32, (8, experts), 0) + g * local
    ) & (lax.broadcasted_iota(jnp.int32, (8, experts), 0) < local)
    pick = pick.astype(f32).astype(bf16)
    halves = []
    for h in range(2):
        total = probs_all[h * half_groups].astype(f32)
        for b in range(1, half_groups):
            total = total + probs_all[h * half_groups + b].astype(f32)
        halves.append(jnp.dot(pick, total.astype(bf16), preferred_element_type=f32))
    lane = lax.broadcasted_iota(jnp.int32, (half_tokens, half_tokens), 1)
    before = lax.broadcasted_iota(jnp.int32, (half_tokens, half_tokens), 0)
    earlier = (before < lane) & (before // rows == lane // rows)
    earlier = earlier.astype(f32).astype(bf16)
    half_block = lax.broadcasted_iota(jnp.int32, (8, half_tokens), 1) // rows
    for h in range(2):
        used = halves[h] > 0.0
        rank = jnp.dot(used.astype(f32).astype(bf16), earlier, preferred_element_type=f32)
        slot = (half_block + h * half_groups) * capacity + rank.astype(jnp.int32)
        slot_ref[h] = jnp.where(used, slot, -1)
    prob_tokens = jnp.concatenate(halves, axis=1)

    def slot_row(l, h):
        table = slot_ref[h]
        mask = lax.broadcasted_iota(jnp.int32, table.shape, 0) == l
        return jnp.sum(jnp.where(mask, table, 0), axis=0, keepdims=True)

    for l in range(local):
        row = jnp.concatenate([slot_row(l, 0), slot_row(l, 1)], axis=1)
        match = lax.broadcasted_iota(jnp.int32, (span, tokens), 0) == row
        prob_col[l] = jnp.sum(
            jnp.where(match, prob_tokens[l : l + 1, :], 0.0), axis=1, keepdims=True
        )

    rows_copy(grad_ref, mate, g, 0).wait_recv()
    for n, peer in enumerate(peers):
        b = peer + 1 - 2 * parity
        rows_copy(grad_ref, b, g, 0).wait_recv()
    for copy in w_copies:
        copy.wait()

    order = [lax.rem(chip + 1 + i, chips) for i in range(chips)]

    def a_copy(l, half, to):
        return pltpu.make_async_remote_copy(
            src_ref=part.at[l, pl.ds(pl.multiple_of(half * share, share), share), :],
            dst_ref=recv_a.at[l], send_sem=a_send.at[l], recv_sem=a_recv.at[l],
            device_id=(g, to), device_id_type=MESH,
        )

    def b_copy(l):
        return pltpu.make_async_remote_copy(
            src_ref=send_b.at[l], dst_ref=recv_b.at[chip],
            send_sem=b_send.at[l], recv_sem=b_recv.at[chip],
            device_id=(g, l * 2 + core), device_id_type=MESH,
        )

    partner = k + 1 - 2 * core
    step = min(width, 256)
    for l in order:
        row = jnp.concatenate([slot_row(l, 0), slot_row(l, 1)], axis=1)
        match = lax.broadcasted_iota(jnp.int32, (span, tokens), 0) == row
        slot_rows[l] = jnp.dot(
            match.astype(f32).astype(bf16), rows_all[...], preferred_element_type=f32
        ).astype(bf16)
        for n in range(0, width, step):
            part[l, :, n : n + step] = jnp.dot(
                slot_rows[l], w_ref[l, :, n : n + step], preferred_element_type=f32
            ).astype(bf16)
        copy = a_copy(l, 1 - core, partner)
        copy.start()
        sends.append(copy)

    saved_copy.wait()
    kept = pl.ds(pl.multiple_of(core * share, share), share)
    for i, l in enumerate(order):
        a_copy(l, 1 - core, partner).wait_recv()
        both = part[l, kept, :].astype(f32) + recv_a[l].astype(f32)
        send_b[l] = both.astype(bf16)
        if i < chips - 1:
            copy = b_copy(l)
            copy.start()
            sends.append(copy)
        start = pl.multiple_of(l * span + core * share, share)
        score = jnp.sum(
            saved_ref[pl.ds(start, share), :].astype(f32) * both, axis=1, keepdims=True
        )
        match = (
            lax.broadcasted_iota(jnp.int32, (share, half_tokens), 0) + core * share
            == slot_row(l, core)
        )
        score_own[pl.ds(l, 1), :] = jnp.sum(jnp.where(match, score, 0.0), axis=0, keepdims=True)

    def score_copy(b, to, sem, y, o):
        return pltpu.make_async_remote_copy(
            src_ref=score_own, dst_ref=score_recv.at[y, o],
            send_sem=sc_send.at[sem], recv_sem=sc_recv.at[y * groups + o],
            device_id=(b, to), device_id_type=MESH,
        )

    for j in range(half_groups):
        b = core * half_groups + j
        for dk in range(parts):
            copy = score_copy(b, lax.rem(k + dk, parts), j * parts + dk, chip, g)
            if dk:
                copy.start()
            else:
                pl.when(b != g)(copy.start)

    my_half = g // half_groups

    @pl.when(my_half == core)
    def _():
        score_recv[chip, g] = score_own[...]

    for l in range(local):
        scaled_ref[l] = (prob_col[l] * slot_rows[l].astype(f32)).astype(bf16)

    for i in range(chips - 1):
        source = order[i]
        pltpu.make_async_remote_copy(
            src_ref=send_b.at[0], dst_ref=recv_b.at[source],
            send_sem=b_send.at[0], recv_sem=b_recv.at[source],
            device_id=(g, k), device_id_type=MESH,
        ).wait_recv()
    total = send_b[chip].astype(f32)
    for i in range(chips - 1):
        total = total + recv_b[order[i]].astype(f32)
    hidden_ref[...] = (prob_col[chip, kept, :] * total).astype(bf16)

    for y in range(chips):
        for o in range(groups):
            wait = score_copy(g, k, 0, y, o).wait_recv
            pl.when((o != g) | (y != chip) | (my_half != core))(wait)
    for o in range(groups):
        value = score_recv[0, o]
        for y in range(1, chips):
            value = value + score_recv[y, o]
        score_rows[o * local : (o + 1) * local, :] = value
    take = (
        lax.broadcasted_iota(jnp.int32, (half_tokens, rows), 0)
        == lax.broadcasted_iota(jnp.int32, (half_tokens, rows), 1) + lane_off
    )
    pair = jnp.dot(
        score_rows[...], take.astype(f32), preferred_element_type=f32,
        precision=lax.Precision.HIGHEST,
    )
    mean = jnp.sum(probs * pair, axis=0, keepdims=True) / route_scale
    terms = jnp.where(named, probs * (1.0 - sig) * (pair - mean), 0.0).astype(bf16)
    eye = (
        lax.broadcasted_iota(jnp.int32, (rows, rows), 0)
        == lax.broadcasted_iota(jnp.int32, (rows, rows), 1)
    )
    turned = lax.dot_general(
        eye.astype(f32).astype(bf16), terms, (((1,), (1,)), ((), ())), preferred_element_type=f32
    ).astype(bf16)
    input_ref[...] = jnp.dot(turned, rw_ref[...], preferred_element_type=f32).astype(bf16)

    for copy in sends:
        copy.wait_send()
    for j in range(half_groups):
        b = core * half_groups + j
        for dk in range(parts):
            wait = score_copy(b, lax.rem(k + dk, parts), j * parts + dk, chip, g).wait_send
            if dk:
                wait()
            else:
                pl.when(b != g)(wait)


def fused(out_grad, expert_ids, router_logits, router_weight, expert_weight, hidden_saved):
    groups, parts = lax.axis_size("grp"), lax.axis_size("ep")
    rows, features = out_grad.shape
    experts = router_logits.shape[1]
    local, _, width = expert_weight.shape
    slots = hidden_saved.shape[1]
    span = slots // local
    half_tokens = groups // 2 * rows
    share = span // 2
    chips = parts // 2
    f32, bf16 = jnp.float32, jnp.bfloat16
    vmem = pl.BlockSpec(memory_space=pltpu.VMEM)
    anyspace = pl.BlockSpec(memory_space=pl.ANY)
    dma = pltpu.SemaphoreType.DMA
    scaled, hidden, input_grad = pl.pallas_call(
        fused_kernel,
        out_shape=(
            jax.ShapeDtypeStruct((local, span, features), bf16),
            jax.ShapeDtypeStruct((share, width), bf16),
            jax.ShapeDtypeStruct((rows, features), bf16),
        ),
        in_specs=[vmem, vmem, vmem, vmem, anyspace, anyspace],
        out_specs=(vmem, vmem, vmem),
        scratch_shapes=[
            pltpu.VMEM((local, features, width), bf16),
            pltpu.VMEM((slots, width), bf16),
            pltpu.VMEM((groups * rows, features), bf16),
            pltpu.VMEM((groups, experts, half_tokens), bf16),
            pltpu.VMEM((experts, half_tokens), bf16),
            pltpu.VMEM((2, 8, half_tokens), jnp.int32),
            pltpu.VMEM((local, span, features), bf16),
            pltpu.VMEM((local, span, 1), f32),
            pltpu.VMEM((local, span, width), bf16),
            pltpu.VMEM((local, share, width), bf16),
            pltpu.VMEM((local, share, width), bf16),
            pltpu.VMEM((chips, share, width), bf16),
            pltpu.VMEM((local, half_tokens), f32),
            pltpu.VMEM((chips, groups, local, half_tokens), f32),
            pltpu.VMEM((experts, half_tokens), f32),
            dma((local,)), dma, dma((groups - 1,)), dma((groups,)),
            dma((groups - 1,)), dma((groups,)),
            dma((local,)), dma((local,)), dma((local,)), dma((chips,)),
            dma((groups // 2 * parts,)), dma((chips * groups,)),
        ],
        compiler_params=pltpu.CompilerParams(
            collective_id=0, has_side_effects=True, vmem_limit_bytes=40 * 1024 * 1024
        ),
    )(
        expert_ids.T, router_logits.T, out_grad, router_weight, expert_weight,
        hidden_saved.reshape(slots, width),
    )
    saved_rows = hidden_saved.reshape(local, span, width)
    weight_grad = jnp.einsum(
        "lmd,lmf->ldf", scaled, saved_rows, preferred_element_type=f32
    ).astype(bf16)
    return weight_grad, hidden[None], input_grad


def choose(*args):
    out_grad, _, _, _, expert_weight, hidden_saved = args
    groups, parts = lax.axis_size("grp"), lax.axis_size("ep")
    rows, local = out_grad.shape[0], expert_weight.shape[0]
    slots_for_one = hidden_saved.shape[1] // groups
    lanes = groups // 2 * rows
    if parts == 2 * local and groups % 2 == 0 and rows <= slots_for_one and lanes % 128 == 0:
        return fused(*args)
    return body(*args)


def solution(mesh):
    in_specs = (
        P("grp", "ep"),
        P("grp", None),
        P("grp", None),
        P(None, "ep"),
        P("grp", "ep", None),
        P("grp", None, None),
    )
    out_specs = (P("grp", "ep", None), P("grp", "ep", None), P("grp", "ep"))
    return jax.shard_map(choose, mesh=mesh, in_specs=in_specs, out_specs=out_specs, check_vma=False)
```

profile of v0, /device:TPU:0, one launch (start us, length us, event | category | flops | bytes accessed | tf_op | source)
XLA Modules:
  0.0 40.4 jit_solution(17395211627296477204)
XLA Ops:
  0.6 0.0 copy-start
  0.6 2.2 %copy-done = bf16[2,1024,1024]{2,1,0:T(8,128)(2,1)S(1)} copy-done((bf16[2,1024,1024]{2,1,0:T(8,128)(2,1)S(1)}, bf16[2,1024,1024]{2,1,0:T(8,128)(2,1)}, u32[]{:S(2)}) %copy-start) | copy-done | bytes 4194328
  2.8 0.0 copy-start.1
  2.8 1.2 %copy-done.1 = bf16[1,512,1024]{2,1,0:T(8,128)(2,1)S(1)} copy-done((bf16[1,512,1024]{2,1,0:T(8,128)(2,1)S(1)}, bf16[1,512,1024]{2,1,0:T(8,128)(2,1)}, u32[]{:S(2)}) %copy-start.1) | copy-done | bytes 1048600
  4.0 0.0 copy-start.2
  4.0 0.8 %copy-done.2 = bf16[32,1024]{1,0:T(8,128)(2,1)S(1)} copy-done((bf16[32,1024]{1,0:T(8,128)(2,1)S(1)}, bf16[32,1024]{1,0:T(8,128)(2,1)}, u32[]{:S(2)}) %copy-start.2) | copy-done | bytes 65560
  4.9 0.0 copy-start.3
  4.9 0.8 %copy-done.3 = bf16[16,1024]{1,0:T(8,128)(2,1)S(1)} copy-done((bf16[16,1024]{1,0:T(8,128)(2,1)S(1)}, bf16[16,1024]{1,0:T(8,128)(2,1)}, u32[]{:S(2)}) %copy-start.3) | copy-done | bytes 32792
  5.6 0.0 copy-start.4
  5.6 0.7 %copy-done.4 = f32[32,16]{0,1:T(8,128)S(1)} copy-done((f32[32,16]{0,1:T(8,128)S(1)}, f32[32,16]{0,1:T(8,128)}, u32[]{:S(2)}) %copy-start.4) | copy-done | bytes 2072
  6.3 0.0 copy-start.5
  6.3 0.7 %copy-done.5 = s32[32,8]{0,1:T(8,128)S(1)} copy-done((s32[32,8]{0,1:T(8,128)S(1)}, s32[32,8]{0,1:T(8,128)}, u32[]{:S(2)}) %copy-start.5) | copy-done | bytes 1048
  7.0 28.8 %shard_map.85 = (bf16[2,256,1024]{2,1,0:T(8,128)(2,1)S(1)}, bf16[128,1024]{1,0:T(8,128)(2,1)S(1)}, bf16[32,1024]{1,0:T(8,128)(2,1)S(1)}) custom-call(s32[8,32]{1,0:T(8,128)S(1)} %bitcast.11, f32[16,32]{1,0:T(8,128)S(1)} %bitcast.10, bf16[32,1024]{1,0:T(8,128)(2,1)S(1)} %copy-done.2, bf16[16,1024]{1,0:T(8,128)(2,1)S(1)} %copy-done.3, ...), custom_call_target="tpu_custom_call" | custom-call | tf_op jit(solution)/shard_map/pallas_call | solution.py:393
  35.8 3.3 %convolution_convert_fusion = bf16[2,1024,1024]{2,1,0:T(8,128)(2,1)} fusion(bf16[2,256,1024]{2,1,0:T(8,128)(2,1)S(1)} %get-tuple-element.6, bf16[2,256,1024]{2,1,0:T(8,128)(2,1)S(1)} %bitcast.8), kind=kOutput, calls=%fused_computation | convolution fusion | flops 1075838976 | bytes 6291456 | tf_op jit(solution)/shard_map/lmd,lmf->ldf/dot_general | solution.py:431
  39.1 0.7 %copy.13 = bf16[1,128,1024]{2,1,0:T(8,128)(2,1)} copy(bf16[1,128,1024]{2,1,0:T(8,128)(2,1)S(1)} %bitcast.9) | data formatting | bytes 524288
  39.8 0.6 %copy.14 = bf16[32,1024]{1,0:T(8,128)(2,1)} copy(bf16[32,1024]{1,0:T(8,128)(2,1)S(1)} %get-tuple-element.14) | data formatting | bytes 131072
Async XLA Ops:
  0.6 2.2 %copy-start = (bf16[2,1024,1024]{2,1,0:T(8,128)(2,1)S(1)}, bf16[2,1024,1024]{2,1,0:T(8,128)(2,1)}, u32[]{:S(2)}) copy-start(bf16[2,1024,1024]{2,1,0:T(8,128)(2,1)} %w_hbm.1) | copy-start | bytes 12582916
  2.8 1.2 %copy-start.1 = (bf16[1,512,1024]{2,1,0:T(8,128)(2,1)S(1)}, bf16[1,512,1024]{2,1,0:T(8,128)(2,1)}, u32[]{:S(2)}) copy-start(bf16[1,512,1024]{2,1,0:T(8,128)(2,1)} %param.11) | copy-start | bytes 3145732
  4.0 0.8 %copy-start.2 = (bf16[32,1024]{1,0:T(8,128)(2,1)S(1)}, bf16[32,1024]{1,0:T(8,128)(2,1)}, u32[]{:S(2)}) copy-start(bf16[32,1024]{1,0:T(8,128)(2,1)} %grad_ref.1) | copy-start | bytes 196612
  4.9 0.8 %copy-start.3 = (bf16[16,1024]{1,0:T(8,128)(2,1)S(1)}, bf16[16,1024]{1,0:T(8,128)(2,1)}, u32[]{:S(2)}) copy-start(bf16[16,1024]{1,0:T(8,128)(2,1)} %rw_ref.1) | copy-start | bytes 98308
  5.6 0.7 %copy-start.4 = (f32[32,16]{0,1:T(8,128)S(1)}, f32[32,16]{0,1:T(8,128)}, u32[]{:S(2)}) copy-start(f32[32,16]{0,1:T(8,128)} %param.8) | copy-start | bytes 6148
  6.3 0.7 %copy-start.5 = (s32[32,8]{0,1:T(8,128)S(1)}, s32[32,8]{0,1:T(8,128)}, u32[]{:S(2)}) copy-start(s32[32,8]{0,1:T(8,128)} %param.7) | copy-start | bytes 3076
where the time goes:
time: 41.2 us; the launch traced here: 40.4 us
  Pallas kernels  28.8 us (70%)
  local copies, waits for them, and re-layouts  7.72 us (19%)
  matrix products  3.32 us (8%)
  between operations  0.65 us (2%)
    pallas_call x1, Pallas kernels, fused(): pl.pallas_call(fused_kernel, out_shape=(jax.ShapeDtypeStruct((local, span...  28.8 us
    unnamed x14, local copies, waits for them, and re-layouts  7.72 us
    dot_general x1, matrix products, fused(): jnp.einsum('lmd,lmf->ldf', scaled, saved_rows, preferred_element_type=f32)  3.32 us

commit v1 on v0

v1 whole, which is shorter than its diff:
```python
import jax
import jax.numpy as jnp
from jax import lax
from jax.experimental import pallas as pl
from jax.experimental.pallas import tpu as pltpu
from jax.sharding import PartitionSpec as P

route_scale = 2.5


def body(out_grad, expert_ids, router_logits, router_weight, expert_weight, hidden_saved):
    group_rows, features = out_grad.shape
    top_count = expert_ids.shape[1]
    experts = router_logits.shape[1]
    group_count = lax.axis_size("grp")
    local_experts = expert_weight.shape[0]
    hidden_width = expert_weight.shape[2]
    slot_count = hidden_saved.shape[1]
    capacity = slot_count // (local_experts * group_count)
    expert_span = group_count * capacity
    pair_count = group_rows * top_count
    sig_values = jax.nn.sigmoid(router_logits)
    picked = expert_ids[:, :, None] == jnp.arange(experts, dtype=jnp.int32)[None, None, :]
    chosen = jnp.sum(jnp.where(picked, sig_values[:, None, :], 0.0), axis=2)
    route_probs = route_scale * chosen / jnp.sum(chosen, axis=1, keepdims=True)
    flat_ids = expert_ids.reshape(pair_count)
    onehot = picked.reshape(pair_count, experts).astype(jnp.int32)
    pair_ranks = jnp.sum((jnp.cumsum(onehot, axis=0) - 1) * onehot, axis=1)
    slot_place = (
        flat_ids % local_experts * group_count + flat_ids // local_experts
    ) * capacity + pair_ranks
    slot_match = slot_place[None, :] == jnp.arange(slot_count, dtype=jnp.int32)[:, None]
    token_pick = jnp.sum(
        slot_match.reshape(slot_count, group_rows, top_count).astype(jnp.float32), axis=2
    ).astype(jnp.bfloat16)
    send_rows = jnp.dot(token_pick, out_grad, preferred_element_type=jnp.float32).astype(
        jnp.bfloat16
    )
    send_prob = jnp.sum(
        jnp.where(slot_match, route_probs.reshape(1, pair_count), 0.0), axis=1
    ).astype(jnp.bfloat16)
    got_rows, got_prob = (
        lax.all_to_all(
            send_rows.reshape(local_experts, group_count, capacity, features),
            "grp",
            split_axis=1,
            concat_axis=1,
            tiled=True,
        ),
        lax.all_to_all(
            send_prob.reshape(local_experts, group_count, capacity),
            "grp",
            split_axis=1,
            concat_axis=1,
            tiled=True,
        ),
    )
    slot_grads = got_rows.reshape(local_experts, expert_span, features)
    prob_rows = got_prob.reshape(local_experts, expert_span).astype(jnp.float32)
    saved_rows = hidden_saved.reshape(local_experts, expert_span, hidden_width)
    scaled_rows = (prob_rows[:, :, None] * slot_grads.astype(jnp.float32)).astype(jnp.bfloat16)
    weight_grad = jnp.einsum(
        "lmd,lmf->ldf", scaled_rows, saved_rows, preferred_element_type=jnp.float32
    ).astype(jnp.bfloat16)
    owner_index = lax.axis_index("ep")
    share_rows = slot_count // lax.axis_size("ep")
    flat_prob = prob_rows.reshape(slot_count)
    flat_saved = hidden_saved.reshape(slot_count, hidden_width)
    partial_term = jnp.einsum(
        "lmd,ldf->lmf", slot_grads, expert_weight, preferred_element_type=jnp.float32
    ).reshape(slot_count, hidden_width)
    rounded_term = lax.optimization_barrier(partial_term.astype(jnp.bfloat16)).astype(jnp.float32)
    partial_score = jnp.sum(flat_saved.astype(jnp.float32) * rounded_term, axis=1)
    moved_scores = lax.all_to_all(
        partial_score.reshape(local_experts, group_count, capacity),
        "grp",
        split_axis=1,
        concat_axis=1,
        tiled=True,
    )
    returned = lax.psum(moved_scores, "ep")
    summed = lax.psum_scatter(
        partial_term.astype(jnp.bfloat16), "ep", scatter_dimension=0, tiled=True
    ).astype(jnp.float32)
    own_prob = lax.dynamic_slice_in_dim(flat_prob, owner_index * share_rows, share_rows, 0)
    hidden_grad = (own_prob[:, None] * summed).astype(jnp.bfloat16)[None]
    pair_score = jnp.sum(
        jnp.where(slot_match, returned.reshape(slot_count, 1), 0.0), axis=0
    ).reshape(group_rows, top_count)
    weighted_mean = jnp.sum(route_probs * pair_score, axis=1, keepdims=True) / route_scale
    logit_terms = route_probs * (1.0 - chosen) * (pair_score - weighted_mean)
    router_grad = jnp.sum(jnp.where(picked, logit_terms[:, :, None], 0.0), axis=1).astype(
        jnp.bfloat16
    )
    input_grad = jnp.dot(router_grad, router_weight, preferred_element_type=jnp.float32).astype(
        jnp.bfloat16
    )
    return (weight_grad, hidden_grad, input_grad)


MESH = pl.DeviceIdType.MESH


def flip(a, j):
    out, bit = a, 1
    while bit <= j:
        if j & bit:
            out = out + bit * (1 - 2 * (a // bit % 2))
        bit *= 2
    return out


def fused_kernel(
    ids_hbm, logits_hbm, grad_hbm, rw_hbm, w_hbm, saved_hbm,
    weight_ref, hidden_ref, input_ref,
    ids_ref, logits_ref, rw_ref, w_ref, saved_ref, rows_all, probs_all, probs_own,
    slot_ref, saved_tok, scaled, part, recv_a, total_own, send_b, recv_b,
    score_own, score_recv, score_rows,
    in_sem, w_sem, rows_send, rows_recv, probs_send, probs_recv,
    a_send, a_recv, b_send, b_recv, sc_send, sc_recv,
):
    groups = lax.axis_size("grp")
    parts = lax.axis_size("ep")
    chips = parts // 2
    g = lax.axis_index("grp")
    k = lax.axis_index("ep")
    chip, core = k // 2, k % 2
    experts, rows = logits_ref.shape
    top = ids_ref.shape[0]
    _, local, _, width = part.shape
    features = rows_all.shape[1]
    half_groups = groups // 2
    half_tokens = half_groups * rows
    tokens = groups * rows
    span = saved_ref.shape[0] // local
    share = span // 2
    capacity = span // groups
    f32, bf16 = jnp.float32, jnp.bfloat16
    i32 = jnp.int32
    column, side = g // 2, lax.rem(g, 2)
    mate = g + 1 - 2 * side
    hops = list(range(half_groups - 1, 0, -1))

    barrier = pltpu.get_barrier_semaphore()
    for dg in range(groups):
        for dk in range(parts):
            if dg or dk:
                pl.semaphore_signal(
                    barrier, inc=1,
                    device_id=(lax.rem(g + dg, groups), lax.rem(k + dk, parts)),
                    device_id_type=MESH,
                )

    def block(b):
        return rows_all.at[pl.ds(pl.multiple_of(b * rows, rows), rows), :]

    fetch = [
        pltpu.make_async_copy(src, dst, in_sem.at[i])
        for i, (src, dst) in enumerate([
            (grad_hbm, block(g)), (logits_hbm, logits_ref), (ids_hbm, ids_ref),
            (saved_hbm, saved_ref), (rw_hbm, rw_ref),
        ])
    ]
    w_copies = [
        pltpu.make_async_copy(w_hbm.at[i], w_ref.at[i], w_sem.at[i]) for i in range(local)
    ]
    for copy in [*fetch[:3], *w_copies, *fetch[3:]]:
        copy.start()

    sends = []

    def go(copy, when=None):
        if when is None:
            copy.start()
            sends.append(copy.wait_send)
        else:
            pl.when(when)(copy.start)
            sends.append(lambda: pl.when(when)(copy.wait_send))

    def rows_copy(b, to, sem):
        return pltpu.make_async_remote_copy(
            src_ref=block(b), dst_ref=block(b), send_sem=rows_send.at[sem],
            recv_sem=rows_recv.at[b], device_id=(to, k), device_id_type=MESH,
        )

    def probs_copy(b, to, sem):
        return pltpu.make_async_remote_copy(
            src_ref=probs_own, dst_ref=probs_all.at[b], send_sem=probs_send.at[sem],
            recv_sem=probs_recv.at[b], device_id=(to, k), device_id_type=MESH,
        )

    fetch[0].wait()
    pl.semaphore_wait(barrier, groups * parts - 1)
    go(rows_copy(g, mate, 0))
    for j in hops:
        go(rows_copy(g, flip(column, j) * 2 + side, j))

    fetch[1].wait()
    fetch[2].wait()
    sig = 1.0 / (1.0 + jnp.exp(-logits_ref[...]))
    ids = ids_ref[...]
    expert_iota = lax.broadcasted_iota(i32, (experts, rows), 0)
    named = ids[0:1, :] == expert_iota
    for i in range(1, top):
        named = named | (ids[i : i + 1, :] == expert_iota)
    probs = route_scale * sig / jnp.sum(jnp.where(named, sig, 0.0), axis=0, keepdims=True)
    probs = jnp.where(named, probs, 0.0)
    lane_off = lax.rem(g, half_groups) * rows
    place = (
        lax.broadcasted_iota(i32, (rows, half_tokens), 1)
        == lax.broadcasted_iota(i32, (rows, half_tokens), 0) + lane_off
    )
    placed = jnp.dot(
        probs.astype(bf16), place.astype(f32).astype(bf16), preferred_element_type=f32
    ).astype(bf16)
    probs_own[...] = placed
    probs_all[g] = placed
    for j in range(1, groups):
        go(probs_copy(g, lax.rem(g + j, groups), j - 1))

    order = [lax.rem(chip + 1 + i, chips) for i in range(chips)]
    partner = k + 1 - 2 * core

    def a_copy(b):
        return pltpu.make_async_remote_copy(
            src_ref=part.at[b], dst_ref=recv_a.at[b], send_sem=a_send.at[b],
            recv_sem=a_recv.at[b], device_id=(g, partner), device_id_type=MESH,
        )

    def own(b):
        return b // half_groups == core

    def multiply(b):
        found = block(b)[...]
        for l in range(local):
            part[b, l] = jnp.dot(found, w_ref[l], preferred_element_type=f32).astype(bf16)
        go(a_copy(b), b // half_groups != core)

    def b_copy(b, l, to, source):
        at = lax.rem(b, half_groups)
        return pltpu.make_async_remote_copy(
            src_ref=send_b.at[l, at], dst_ref=recv_b.at[source, at],
            send_sem=b_send.at[l, at], recv_sem=b_recv.at[source, at],
            device_id=(g, to), device_id_type=MESH,
        )

    def finish(b):
        at = lax.rem(b, half_groups)

        @pl.when(own(b))
        def _():
            a_copy(b).wait_recv()
            for l in order[:-1]:
                both = part[b, l].astype(f32) + recv_a[b, l].astype(f32)
                send_b[l, at] = both.astype(bf16)
                b_copy(b, l, l * 2 + core, chip).start()
            total_own[at] = part[b, chip].astype(f32) + recv_a[b, chip].astype(f32)

        def end():
            for l in order[:-1]:
                b_copy(b, l, l * 2 + core, chip).wait_send()

        sends.append(lambda: pl.when(own(b))(end))

    eye = (
        lax.broadcasted_iota(i32, (rows, half_tokens), 0)
        == lax.broadcasted_iota(i32, (rows, half_tokens), 1)
    )

    def score_copy(b, to, y, o):
        return pltpu.make_async_remote_copy(
            src_ref=score_own.at[b], dst_ref=score_recv.at[y, o],
            send_sem=sc_send.at[b, to], recv_sem=sc_recv.at[y, o],
            device_id=(b, to), device_id_type=MESH,
        )

    def score(b, home=False):
        for l in range(local):
            at = pl.ds(pl.multiple_of(b * rows, rows), rows)
            value = jnp.sum(
                saved_tok[l, at, :].astype(f32) * part[b, l].astype(f32), axis=1, keepdims=True
            )
            score_own[b, l : l + 1, :] = jnp.sum(
                jnp.where(eye, value, 0.0), axis=0, keepdims=True
            )
        if home:
            score_recv[k, b] = score_own[b]
        for dk in range(1 if home else 0, parts):
            go(score_copy(b, lax.rem(k + dk, parts), k, g))

    for copy in w_copies:
        copy.wait()
    multiply(g)

    for j in range(1, groups):
        b = lax.rem(g + j, groups)
        probs_copy(b, g, 0).wait_recv()
    pick = (
        lax.broadcasted_iota(i32, (8, experts), 1)
        == lax.broadcasted_iota(i32, (8, experts), 0) + g * local
    ) & (lax.broadcasted_iota(i32, (8, experts), 0) < local)
    pick = pick.astype(f32).astype(bf16)
    lane = lax.broadcasted_iota(i32, (half_tokens, half_tokens), 1)
    line = lax.broadcasted_iota(i32, (half_tokens, half_tokens), 0)
    same = line // rows == lane // rows
    earlier = ((line < lane) & same).astype(f32).astype(bf16)
    later = ((lane < line) & same).astype(f32).astype(bf16)
    unit = (lane == line).astype(f32).astype(bf16)
    lane_block = lax.broadcasted_iota(i32, (8, half_tokens), 1) // rows
    line_block = lax.broadcasted_iota(i32, (half_tokens, 8), 0) // rows
    turn = (((1,), (1,)), ((), ()))
    fetch[3].wait()
    for h in range(2):
        total = probs_all[h * half_groups].astype(f32)
        for b in range(1, half_groups):
            total = total + probs_all[h * half_groups + b].astype(f32)
        mine = jnp.dot(pick, total.astype(bf16), preferred_element_type=f32)
        used = mine > 0.0
        marks = used.astype(f32).astype(bf16)
        rank = jnp.dot(marks, earlier, preferred_element_type=f32)
        slot = lane_block * capacity + rank.astype(i32)
        slot_ref[h, 0] = jnp.where(used, slot, -1).astype(f32)
        slot_ref[h, 1] = mine
        mine_col = lax.dot_general(unit, mine.astype(bf16), turn, preferred_element_type=f32)
        rank_col = lax.dot_general(later, marks, turn, preferred_element_type=f32)
        slot_col = jnp.where(
            mine_col > 0.0, line_block * capacity + rank_col.astype(i32), -1
        )
        spot = lax.broadcasted_iota(i32, (half_tokens, share), 1)
        at = pl.ds(h * half_tokens, half_tokens)
        for l in range(local):
            match = (slot_col[:, l : l + 1] == spot).astype(f32).astype(bf16)
            start = l * span + h * share
            saved_tok[l, at, :] = jnp.dot(
                match, saved_ref[start : start + share, :], preferred_element_type=f32
            ).astype(bf16)
            scaled[l, at, :] = jnp.broadcast_to(
                mine_col[:, l : l + 1], (half_tokens, scaled.shape[2])
            )

    rows_copy(mate, g, 0).wait_recv()
    multiply(mate)
    score(g, home=True)
    finish(g)
    score(mate)
    last = mate
    for j in hops:
        b = flip(column, j) * 2 + side
        rows_copy(b, g, 0).wait_recv()
        go(rows_copy(b, mate, half_groups + j))
        multiply(b)
        finish(last)
        score(b)
        last = b
    for j in hops:
        b = flip(column, j) * 2 + 1 - side
        rows_copy(b, g, 0).wait_recv()
        multiply(b)
        finish(last)
        score(b)
        last = b

    step = min(width, 256)
    for l in range(local):
        weighed = jnp.concatenate(
            [
                (scaled[l, :, 0:128] * rows_all[:, n : n + 128].astype(f32)).astype(bf16)
                for n in range(0, features, 128)
            ],
            axis=1,
        )
        for n in range(0, width, step):
            weight_ref[l, :, n : n + step] = lax.dot_general(
                weighed, saved_tok[l, :, n : n + step], (((0,), (0,)), ((), ())),
                preferred_element_type=f32,
            ).astype(bf16)
        if l == 0:
            finish(last)

    def pick_row(which):
        table = slot_ref[core, which]
        mask = lax.broadcasted_iota(i32, table.shape, 0) == chip
        return jnp.sum(jnp.where(mask, table, 0.0), axis=0, keepdims=True)

    spot = lax.broadcasted_iota(i32, (share, half_tokens), 0).astype(f32)
    spread = jnp.where(spot == pick_row(0), pick_row(1), 0.0).astype(bf16)
    for i in range(chips - 1):
        for at in range(half_groups):
            b_copy(at, 0, k, order[i]).wait_recv()
    total = total_own[...]
    for i in range(chips - 1):
        total = total + recv_b[order[i]].astype(f32)
    hidden_ref[...] = jnp.dot(
        spread, total.reshape(half_tokens, width).astype(bf16), preferred_element_type=f32
    ).astype(bf16)

    for y in range(parts):
        for o in range(groups):
            wait = score_copy(g, k, y, o).wait_recv
            pl.when((o != g) | (y != k))(wait)
    for o in range(groups):
        value = score_recv[0, o]
        for y in range(1, parts):
            value = value + score_recv[y, o]
        score_rows[o * local : (o + 1) * local, :] = value
    pair = score_rows[:, 0:rows]
    mean = jnp.sum(probs * pair, axis=0, keepdims=True) / route_scale
    terms = jnp.where(named, probs * (1.0 - sig) * (pair - mean), 0.0).astype(bf16)
    small = (
        lax.broadcasted_iota(i32, (rows, rows), 0) == lax.broadcasted_iota(i32, (rows, rows), 1)
    )
    turned = lax.dot_general(
        small.astype(f32).astype(bf16), terms, turn, preferred_element_type=f32
    ).astype(bf16)
    fetch[4].wait()
    input_ref[...] = jnp.dot(turned, rw_ref[...], preferred_element_type=f32).astype(bf16)

    for wait in sends:
        wait()


def write_kernel(weight_ref, hidden_ref, input_ref, weight_hbm, hidden_hbm, input_hbm, sem):
    copies = [
        pltpu.make_async_copy(hidden_ref, hidden_hbm, sem.at[0]),
        pltpu.make_async_copy(input_ref, input_hbm, sem.at[1]),
    ]
    local, features, _ = weight_ref.shape
    cut = features // 4
    for l in range(local):
        for n in range(4):
            at = pl.ds(n * cut, cut)
            copies.append(
                pltpu.make_async_copy(
                    weight_ref.at[l, at, :], weight_hbm.at[l, at, :], sem.at[2 + l * 4 + n]
                )
            )
    for copy in copies:
        copy.start()
    for copy in copies:
        copy.wait()


def fused(out_grad, expert_ids, router_logits, router_weight, expert_weight, hidden_saved):
    groups, parts = lax.axis_size("grp"), lax.axis_size("ep")
    rows, features = out_grad.shape
    experts = router_logits.shape[1]
    top = expert_ids.shape[1]
    local, _, width = expert_weight.shape
    slots = hidden_saved.shape[1]
    span = slots // local
    half_groups = groups // 2
    half_tokens = half_groups * rows
    tokens = groups * rows
    share = span // 2
    chips = parts // 2
    f32, bf16 = jnp.float32, jnp.bfloat16
    vmem = pl.BlockSpec(memory_space=pltpu.VMEM)
    hbm = pl.BlockSpec(memory_space=pltpu.HBM)
    dma = pltpu.SemaphoreType.DMA
    out_shape = (
        jax.ShapeDtypeStruct((local, features, width), bf16),
        jax.ShapeDtypeStruct((share, width), bf16),
        jax.ShapeDtypeStruct((rows, features), bf16),
    )
    outs = pl.pallas_call(
        fused_kernel,
        out_shape=out_shape,
        in_specs=[hbm] * 6,
        out_specs=(vmem, vmem, vmem),
        scratch_shapes=[
            pltpu.VMEM((top, rows), jnp.int32),
            pltpu.VMEM((experts, rows), f32),
            pltpu.VMEM((experts, features), bf16),
            pltpu.VMEM((local, features, width), bf16),
            pltpu.VMEM((slots, width), bf16),
            pltpu.VMEM((tokens, features), bf16),
            pltpu.VMEM((groups, experts, half_tokens), bf16),
            pltpu.VMEM((experts, half_tokens), bf16),
            pltpu.VMEM((2, 2, 8, half_tokens), f32),
            pltpu.VMEM((local, tokens, width), bf16),
            pltpu.VMEM((local, tokens, 128), f32),
            pltpu.VMEM((groups, local, rows, width), bf16),
            pltpu.VMEM((groups, local, rows, width), bf16),
            pltpu.VMEM((half_groups, rows, width), f32),
            pltpu.VMEM((local, half_groups, rows, width), bf16),
            pltpu.VMEM((chips, half_groups, rows, width), bf16),
            pltpu.VMEM((groups, local, half_tokens), f32),
            pltpu.VMEM((parts, groups, local, half_tokens), f32),
            pltpu.VMEM((experts, half_tokens), f32),
            dma((5,)), dma((local,)), dma((2 * half_groups,)), dma((groups,)),
            dma((groups - 1,)), dma((groups,)),
            dma((groups,)), dma((groups,)),
            dma((local, half_groups)), dma((chips, half_groups)),
            dma((groups, parts)), dma((parts, groups)),
        ],
        compiler_params=pltpu.CompilerParams(
            collective_id=0, has_side_effects=True, vmem_limit_bytes=40 * 1024 * 1024
        ),
    )(
        expert_ids.T, router_logits.T, out_grad, router_weight, expert_weight,
        hidden_saved.reshape(slots, width),
    )
    weight_grad, hidden, input_grad = pl.pallas_call(
        write_kernel,
        out_shape=out_shape,
        in_specs=[vmem] * 3,
        out_specs=[hbm] * 3,
        scratch_shapes=[dma((2 + 4 * local,))],
    )(*outs)
    return weight_grad, hidden[None], input_grad


def choose(*args):
    out_grad, _, _, _, expert_weight, hidden_saved = args
    groups, parts = lax.axis_size("grp"), lax.axis_size("ep")
    rows, local = out_grad.shape[0], expert_weight.shape[0]
    slots_for_one = hidden_saved.shape[1] // groups
    lanes = groups // 2 * rows
    capacity = slots_for_one // local
    fits = rows <= capacity and lanes % 128 == 0 and lanes <= 256 and local <= 8
    if parts == 2 * local and groups % 2 == 0 and fits and groups & (groups - 1) == 0:
        return fused(*args)
    return body(*args)


def solution(mesh):
    in_specs = (
        P("grp", "ep"),
        P("grp", None),
        P("grp", None),
        P(None, "ep"),
        P("grp", "ep", None),
        P("grp", None, None),
    )
    out_specs = (P("grp", "ep", None), P("grp", "ep", None), P("grp", "ep"))
    return jax.shard_map(choose, mesh=mesh, in_specs=in_specs, out_specs=out_specs, check_vma=False)
```

time: 41.2 us -> 45.2 us (1.097)
  Pallas kernels: 28.8 us -> 34.5 us
  matrix products: 3.32 us -> 0 us
  local copies, waits for them, and re-layouts: 7.72 us -> 9.66 us
    pallas_call x1 -> x2, Pallas kernels: 28.8 us -> 34.5 us  [the longest x1 30 us: fused(): pl.pallas_call(fused_kernel, out_shape=out_shape, in_specs=[hbm] * 6, out...]
    dot_general x1 -> x0, matrix products: 3.32 us -> none  [fused(): jnp.einsum('lmd,lmf->ldf', scaled, saved_rows, preferred_element_type=f32)]
    unnamed x14 -> x18, local copies, waits for them, and re-layouts: 7.72 us -> 9.66 us
where the time goes in v1:
time: 45.2 us; the launch traced here: 44.8 us
  Pallas kernels  34.5 us (76%)
  local copies, waits for them, and re-layouts  9.66 us (21%)
  between operations  0.66 us (1%)
    pallas_call x1, Pallas kernels, fused(): pl.pallas_call(fused_kernel, out_shape=out_shape, in_specs=[hbm] * 6, out...  30 us
    unnamed x18, local copies, waits for them, and re-layouts  9.66 us
    pallas_call x1, Pallas kernels, fused(): pl.pallas_call(write_kernel, out_shape=out_shape, in_specs=[vmem] * 3, ou...  4.47 us

profile of v1, /device:TPU:0, one launch (start us, length us, event | category | flops | bytes accessed | tf_op | source)
XLA Modules:
  0.0 44.8 jit_solution(4350920293715927125)
XLA Ops:
  0.6 0.0 copy-start
  0.6 2.2 %copy-done = bf16[2,1024,1024]{2,1,0:T(8,128)(2,1)S(1)} copy-done((bf16[2,1024,1024]{2,1,0:T(8,128)(2,1)S(1)}, bf16[2,1024,1024]{2,1,0:T(8,128)(2,1)}, u32[]{:S(2)}) %copy-start) | copy-done | bytes 4194328
  2.8 0.0 copy-start.2
  2.8 1.2 %copy-done.2 = bf16[1,512,1024]{2,1,0:T(8,128)(2,1)S(1)} copy-done((bf16[1,512,1024]{2,1,0:T(8,128)(2,1)S(1)}, bf16[1,512,1024]{2,1,0:T(8,128)(2,1)}, u32[]{:S(2)}) %copy-start.2) | copy-done | bytes 1048600
  4.0 0.0 copy-start.4
  4.0 0.8 %copy-done.4 = bf16[32,1024]{1,0:T(8,128)(2,1)S(1)} copy-done((bf16[32,1024]{1,0:T(8,128)(2,1)S(1)}, bf16[32,1024]{1,0:T(8,128)(2,1)}, u32[]{:S(2)}) %copy-start.4) | copy-done | bytes 65560
  4.9 0.0 copy-start.6
  4.9 0.8 %copy-done.6 = bf16[16,1024]{1,0:T(8,128)(2,1)S(1)} copy-done((bf16[16,1024]{1,0:T(8,128)(2,1)S(1)}, bf16[16,1024]{1,0:T(8,128)(2,1)}, u32[]{:S(2)}) %copy-start.6) | copy-done | bytes 32792
  5.6 0.0 copy-start.7
  5.6 0.7 %copy-done.7 = f32[32,16]{0,1:T(8,128)S(1)} copy-done((f32[32,16]{0,1:T(8,128)S(1)}, f32[32,16]{0,1:T(8,128)}, u32[]{:S(2)}) %copy-start.7) | copy-done | bytes 2072
  6.3 0.0 copy-start.8
  6.3 0.7 %copy-done.8 = s32[32,8]{0,1:T(8,128)S(1)} copy-done((s32[32,8]{0,1:T(8,128)S(1)}, s32[32,8]{0,1:T(8,128)}, u32[]{:S(2)}) %copy-start.8) | copy-done | bytes 1048
  7.0 30.0 %shard_map.85 = (bf16[2,1024,1024]{2,1,0:T(8,128)(2,1)S(1)}, bf16[128,1024]{1,0:T(8,128)(2,1)S(1)}, bf16[32,1024]{1,0:T(8,128)(2,1)S(1)}) custom-call(s32[8,32]{1,0:T(8,128)S(1)} %bitcast.6, f32[16,32]{1,0:T(8,128)S(1)} %bitcast.5, bf16[32,1024]{1,0:T(8,128)(2,1)S(1)} %copy-done.4, bf16[16,1024]{1,0:T(8,128)(2,1)S(1)} %copy-done.6, ...), custom_call_target="tpu_custom_call" | custom-call | tf_op jit(solution)/shard_map/pallas_call | solution.py:465
  37.0 0.0 copy-start.1
  37.0 1.9 %copy-done.1 = bf16[2,1024,1024]{2,1,0:T(8,128)(2,1)} copy-done((bf16[2,1024,1024]{2,1,0:T(8,128)(2,1)}, bf16[2,1024,1024]{2,1,0:T(8,128)(2,1)S(1)}, u32[]{:S(2)}) %copy-start.1) | copy-done | bytes 4194328
  39.0 0.0 copy-start.3
  39.0 0.7 %copy-done.3 = bf16[128,1024]{1,0:T(8,128)(2,1)} copy-done((bf16[128,1024]{1,0:T(8,128)(2,1)}, bf16[128,1024]{1,0:T(8,128)(2,1)S(1)}, u32[]{:S(2)}) %copy-start.3) | copy-done | bytes 262168
  39.7 0.0 copy-start.5
  39.7 0.6 %copy-done.5 = bf16[32,1024]{1,0:T(8,128)(2,1)} copy-done((bf16[32,1024]{1,0:T(8,128)(2,1)}, bf16[32,1024]{1,0:T(8,128)(2,1)S(1)}, u32[]{:S(2)}) %copy-start.5) | copy-done | bytes 65560
  40.3 4.5 %shard_map.86 = (bf16[2,1024,1024]{2,1,0:T(8,128)(2,1)}, bf16[128,1024]{1,0:T(8,128)(2,1)}, bf16[32,1024]{1,0:T(8,128)(2,1)}) custom-call(bf16[2,1024,1024]{2,1,0:T(8,128)(2,1)} %copy-done.1, bf16[128,1024]{1,0:T(8,128)(2,1)} %copy-done.3, bf16[32,1024]{1,0:T(8,128)(2,1)} %copy-done.5), custom_call_target="tpu_custom_call" | custom-call | tf_op jit(solution)/shard_map/pallas_call | solution.py:503
Async XLA Ops:
  0.6 2.2 %copy-start = (bf16[2,1024,1024]{2,1,0:T(8,128)(2,1)S(1)}, bf16[2,1024,1024]{2,1,0:T(8,128)(2,1)}, u32[]{:S(2)}) copy-start(bf16[2,1024,1024]{2,1,0:T(8,128)(2,1)} %w_hbm.1) | copy-start | bytes 12582916
  2.8 1.2 %copy-start.2 = (bf16[1,512,1024]{2,1,0:T(8,128)(2,1)S(1)}, bf16[1,512,1024]{2,1,0:T(8,128)(2,1)}, u32[]{:S(2)}) copy-start(bf16[1,512,1024]{2,1,0:T(8,128)(2,1)} %param.11) | copy-start | bytes 3145732
  4.0 0.8 %copy-start.4 = (bf16[32,1024]{1,0:T(8,128)(2,1)S(1)}, bf16[32,1024]{1,0:T(8,128)(2,1)}, u32[]{:S(2)}) copy-start(bf16[32,1024]{1,0:T(8,128)(2,1)} %grad_hbm.1) | copy-start | bytes 196612
  4.9 0.8 %copy-start.6 = (bf16[16,1024]{1,0:T(8,128)(2,1)S(1)}, bf16[16,1024]{1,0:T(8,128)(2,1)}, u32[]{:S(2)}) copy-start(bf16[16,1024]{1,0:T(8,128)(2,1)} %rw_hbm.1) | copy-start | bytes 98308
  5.6 0.7 %copy-start.7 = (f32[32,16]{0,1:T(8,128)S(1)}, f32[32,16]{0,1:T(8,128)}, u32[]{:S(2)}) copy-start(f32[32,16]{0,1:T(8,128)} %param.8) | copy-start | bytes 6148
  6.3 0.7 %copy-start.8 = (s32[32,8]{0,1:T(8,128)S(1)}, s32[32,8]{0,1:T(8,128)}, u32[]{:S(2)}) copy-start(s32[32,8]{0,1:T(8,128)} %param.7) | copy-start | bytes 3076
  37.0 1.9 %copy-start.1 = (bf16[2,1024,1024]{2,1,0:T(8,128)(2,1)}, bf16[2,1024,1024]{2,1,0:T(8,128)(2,1)S(1)}, u32[]{:S(2)}) copy-start(bf16[2,1024,1024]{2,1,0:T(8,128)(2,1)S(1)} %get-tuple-element.9.weight_ref) | copy-start | bytes 12582916
  39.0 0.7 %copy-start.3 = (bf16[128,1024]{1,0:T(8,128)(2,1)}, bf16[128,1024]{1,0:T(8,128)(2,1)S(1)}, u32[]{:S(2)}) copy-start(bf16[128,1024]{1,0:T(8,128)(2,1)S(1)} %get-tuple-element.10.hidden_ref) | copy-start | bytes 786436
  39.7 0.6 %copy-start.5 = (bf16[32,1024]{1,0:T(8,128)(2,1)}, bf16[32,1024]{1,0:T(8,128)(2,1)S(1)}, u32[]{:S(2)}) copy-start(bf16[32,1024]{1,0:T(8,128)(2,1)S(1)} %get-tuple-element.11.input_ref) | copy-start | bytes 196612

commit v2 on v1

--- a/solution.py
+++ b/solution.py
@@ -462,9 +462,10 @@
         jax.ShapeDtypeStruct((share, width), bf16),
         jax.ShapeDtypeStruct((rows, features), bf16),
     )
+    pin = pltpu.with_memory_space_constraint
     outs = pl.pallas_call(
         fused_kernel,
-        out_shape=out_shape,
+        out_shape=tuple(pltpu.VMEM(x.shape, x.dtype) for x in out_shape),
         in_specs=[hbm] * 6,
         out_specs=(vmem, vmem, vmem),
         scratch_shapes=[
@@ -496,17 +497,21 @@
         compiler_params=pltpu.CompilerParams(
             collective_id=0, has_side_effects=True, vmem_limit_bytes=40 * 1024 * 1024
         ),
-    )(
-        expert_ids.T, router_logits.T, out_grad, router_weight, expert_weight,
-        hidden_saved.reshape(slots, width),
-    )
+    )(*[
+        pin(x, pltpu.HBM)
+        for x in (
+            expert_ids.T, router_logits.T, out_grad, router_weight, expert_weight,
+            hidden_saved.reshape(slots, width),
+        )
+    ])
     weight_grad, hidden, input_grad = pl.pallas_call(
         write_kernel,
         out_shape=out_shape,
         in_specs=[vmem] * 3,
         out_specs=[hbm] * 3,
         scratch_shapes=[dma((2 + 4 * local,))],
-    )(*outs)
+        compiler_params=pltpu.CompilerParams(vmem_limit_bytes=16 * 1024 * 1024),
+    )(*[pin(x, pltpu.VMEM) for x in outs])
     return weight_grad, hidden[None], input_grad
 
 

time: 45.2 us -> 33.1 us (0.73)
  local copies, waits for them, and re-layouts: 9.66 us -> 0 us
  Pallas kernels: 34.5 us -> 32.4 us
    unnamed x18 -> x0, local copies, waits for them, and re-layouts: 9.66 us -> none
    pallas_call x1, Pallas kernels: 4.47 us -> 2.2 us  [fused(): pl.pallas_call(write_kernel, out_shape=out_shape, in_specs=[vmem] * 3, ou...]
where the time goes in v2:
time: 33.1 us; the launch traced here: 33 us
  Pallas kernels  32.4 us (98%)
  between operations  0.64 us (2%)
    pallas_call x1, Pallas kernels, fused(): pl.pallas_call(fused_kernel, out_shape=tuple((pltpu.VMEM(x.shape, x.dtype...  30.2 us
    pallas_call x1, Pallas kernels, fused(): pl.pallas_call(write_kernel, out_shape=out_shape, in_specs=[vmem] * 3, ou...  2.2 us

profile of v2, /device:TPU:0, one launch (start us, length us, event | category | flops | bytes accessed | tf_op | source)
XLA Modules:
  0.0 33.0 jit_solution(13304247643089422875)
XLA Ops:
  0.6 30.2 %shard_map.85 = (bf16[2,1024,1024]{2,1,0:T(8,128)(2,1)S(1)}, bf16[128,1024]{1,0:T(8,128)(2,1)S(1)}, bf16[32,1024]{1,0:T(8,128)(2,1)S(1)}) custom-call(s32[8,32]{1,0:T(8,128)} %bitcast.6, f32[16,32]{1,0:T(8,128)} %bitcast.5, bf16[32,1024]{1,0:T(8,128)(2,1)} %grad_hbm.1, bf16[16,1024]{1,0:T(8,128)(2,1)} %rw_hbm.1, bf16[2,1024,1024]{2,1,0:T(8,128)(2,1)} %w_hbm.1, ...), custom_call_target="tpu_custom_call" | custom-call | tf_op jit(solution)/shard_map/pallas_call | solution.py:466
  30.8 2.2 %shard_map.86 = (bf16[2,1024,1024]{2,1,0:T(8,128)(2,1)}, bf16[128,1024]{1,0:T(8,128)(2,1)}, bf16[32,1024]{1,0:T(8,128)(2,1)}) custom-call(bf16[2,1024,1024]{2,1,0:T(8,128)(2,1)S(1)} %get-tuple-element.9.weight_ref, bf16[128,1024]{1,0:T(8,128)(2,1)S(1)} %get-tuple-element.10.hidden_ref, bf16[32,1024]{1,0:T(8,128)(2,1)S(1)} %get-tuple-element.11.input_ref), custom_call_target="tpu_custom_call" | custom-call | tf_op jit(solution)/shard_map/pallas_call | solution.py:507

commit v3 on v2

--- a/solution.py
+++ b/solution.py
@@ -142,14 +142,10 @@
     hops = list(range(half_groups - 1, 0, -1))
 
     barrier = pltpu.get_barrier_semaphore()
-    for dg in range(groups):
-        for dk in range(parts):
-            if dg or dk:
-                pl.semaphore_signal(
-                    barrier, inc=1,
-                    device_id=(lax.rem(g + dg, groups), lax.rem(k + dk, parts)),
-                    device_id_type=MESH,
-                )
+    peers = [(lax.rem(g + j, groups), k) for j in range(1, groups)]
+    peers += [(g, lax.rem(k + j, parts)) for j in range(1, parts)]
+    for peer in peers:
+        pl.semaphore_signal(barrier, inc=1, device_id=peer, device_id_type=MESH)
 
     def block(b):
         return rows_all.at[pl.ds(pl.multiple_of(b * rows, rows), rows), :]
@@ -164,7 +160,7 @@
     w_copies = [
         pltpu.make_async_copy(w_hbm.at[i], w_ref.at[i], w_sem.at[i]) for i in range(local)
     ]
-    for copy in [*fetch[:3], *w_copies, *fetch[3:]]:
+    for copy in [*fetch[1:3], fetch[0], *w_copies, *fetch[3:]]:
         copy.start()
 
     sends = []
@@ -188,12 +184,6 @@
             src_ref=probs_own, dst_ref=probs_all.at[b], send_sem=probs_send.at[sem],
             recv_sem=probs_recv.at[b], device_id=(to, k), device_id_type=MESH,
         )
-
-    fetch[0].wait()
-    pl.semaphore_wait(barrier, groups * parts - 1)
-    go(rows_copy(g, mate, 0))
-    for j in hops:
-        go(rows_copy(g, flip(column, j) * 2 + side, j))
 
     fetch[1].wait()
     fetch[2].wait()
@@ -215,8 +205,13 @@
     ).astype(bf16)
     probs_own[...] = placed
     probs_all[g] = placed
+    fetch[0].wait()
+    pl.semaphore_wait(barrier, len(peers))
     for j in range(1, groups):
         go(probs_copy(g, lax.rem(g + j, groups), j - 1))
+    go(rows_copy(g, mate, 0))
+    for j in hops:
+        go(rows_copy(g, flip(column, j) * 2 + side, j))
 
     order = [lax.rem(chip + 1 + i, chips) for i in range(chips)]
     partner = k + 1 - 2 * core

time: 33.1 us -> 28.3 us (0.85)
  Pallas kernels: 32.4 us -> 27.5 us
    pallas_call x1, Pallas kernels: 30.2 us -> 25.3 us  [fused(): pl.pallas_call(fused_kernel, out_shape=tuple((pltpu.VMEM(x.shape, x.dtype...]
where the time goes in v3:
time: 28.3 us; the launch traced here: 28.1 us
  Pallas kernels  27.5 us (97%)
  between operations  0.64 us (2%)
    pallas_call x1, Pallas kernels, fused(): pl.pallas_call(fused_kernel, out_shape=tuple((pltpu.VMEM(x.shape, x.dtype...  25.3 us
    pallas_call x1, Pallas kernels, fused(): pl.pallas_call(write_kernel, out_shape=out_shape, in_specs=[vmem] * 3, ou...  2.2 us

profile of v3, /device:TPU:0, one launch (start us, length us, event | category | flops | bytes accessed | tf_op | source)
XLA Modules:
  0.0 28.1 jit_solution(1043463544776166227)
XLA Ops:
  0.6 25.3 %shard_map.85 = (bf16[2,1024,1024]{2,1,0:T(8,128)(2,1)S(1)}, bf16[128,1024]{1,0:T(8,128)(2,1)S(1)}, bf16[32,1024]{1,0:T(8,128)(2,1)S(1)}) custom-call(s32[8,32]{1,0:T(8,128)} %bitcast.6, f32[16,32]{1,0:T(8,128)} %bitcast.5, bf16[32,1024]{1,0:T(8,128)(2,1)} %grad_hbm.1, bf16[16,1024]{1,0:T(8,128)(2,1)} %rw_hbm.1, bf16[2,1024,1024]{2,1,0:T(8,128)(2,1)} %w_hbm.1, ...), custom_call_target="tpu_custom_call" | custom-call | tf_op jit(solution)/shard_map/pallas_call | solution.py:461
  25.9 2.2 %shard_map.86 = (bf16[2,1024,1024]{2,1,0:T(8,128)(2,1)}, bf16[128,1024]{1,0:T(8,128)(2,1)}, bf16[32,1024]{1,0:T(8,128)(2,1)}) custom-call(bf16[2,1024,1024]{2,1,0:T(8,128)(2,1)S(1)} %get-tuple-element.9.weight_ref, bf16[128,1024]{1,0:T(8,128)(2,1)S(1)} %get-tuple-element.10.hidden_ref, bf16[32,1024]{1,0:T(8,128)(2,1)S(1)} %get-tuple-element.11.input_ref), custom_call_target="tpu_custom_call" | custom-call | tf_op jit(solution)/shard_map/pallas_call | solution.py:502

commit v4 on v3

v4 whole, which is shorter than its diff:
```python
import jax
import jax.numpy as jnp
from jax import lax
from jax.experimental import pallas as pl
from jax.experimental.pallas import tpu as pltpu
from jax.sharding import PartitionSpec as P

route_scale = 2.5


def body(out_grad, expert_ids, router_logits, router_weight, expert_weight, hidden_saved):
    group_rows, features = out_grad.shape
    top_count = expert_ids.shape[1]
    experts = router_logits.shape[1]
    group_count = lax.axis_size("grp")
    local_experts = expert_weight.shape[0]
    hidden_width = expert_weight.shape[2]
    slot_count = hidden_saved.shape[1]
    capacity = slot_count // (local_experts * group_count)
    expert_span = group_count * capacity
    pair_count = group_rows * top_count
    sig_values = jax.nn.sigmoid(router_logits)
    picked = expert_ids[:, :, None] == jnp.arange(experts, dtype=jnp.int32)[None, None, :]
    chosen = jnp.sum(jnp.where(picked, sig_values[:, None, :], 0.0), axis=2)
    route_probs = route_scale * chosen / jnp.sum(chosen, axis=1, keepdims=True)
    flat_ids = expert_ids.reshape(pair_count)
    onehot = picked.reshape(pair_count, experts).astype(jnp.int32)
    pair_ranks = jnp.sum((jnp.cumsum(onehot, axis=0) - 1) * onehot, axis=1)
    slot_place = (
        flat_ids % local_experts * group_count + flat_ids // local_experts
    ) * capacity + pair_ranks
    slot_match = slot_place[None, :] == jnp.arange(slot_count, dtype=jnp.int32)[:, None]
    token_pick = jnp.sum(
        slot_match.reshape(slot_count, group_rows, top_count).astype(jnp.float32), axis=2
    ).astype(jnp.bfloat16)
    send_rows = jnp.dot(token_pick, out_grad, preferred_element_type=jnp.float32).astype(
        jnp.bfloat16
    )
    send_prob = jnp.sum(
        jnp.where(slot_match, route_probs.reshape(1, pair_count), 0.0), axis=1
    ).astype(jnp.bfloat16)
    got_rows, got_prob = (
        lax.all_to_all(
            send_rows.reshape(local_experts, group_count, capacity, features),
            "grp",
            split_axis=1,
            concat_axis=1,
            tiled=True,
        ),
        lax.all_to_all(
            send_prob.reshape(local_experts, group_count, capacity),
            "grp",
            split_axis=1,
            concat_axis=1,
            tiled=True,
        ),
    )
    slot_grads = got_rows.reshape(local_experts, expert_span, features)
    prob_rows = got_prob.reshape(local_experts, expert_span).astype(jnp.float32)
    saved_rows = hidden_saved.reshape(local_experts, expert_span, hidden_width)
    scaled_rows = (prob_rows[:, :, None] * slot_grads.astype(jnp.float32)).astype(jnp.bfloat16)
    weight_grad = jnp.einsum(
        "lmd,lmf->ldf", scaled_rows, saved_rows, preferred_element_type=jnp.float32
    ).astype(jnp.bfloat16)
    owner_index = lax.axis_index("ep")
    share_rows = slot_count // lax.axis_size("ep")
    flat_prob = prob_rows.reshape(slot_count)
    flat_saved = hidden_saved.reshape(slot_count, hidden_width)
    partial_term = jnp.einsum(
        "lmd,ldf->lmf", slot_grads, expert_weight, preferred_element_type=jnp.float32
    ).reshape(slot_count, hidden_width)
    rounded_term = lax.optimization_barrier(partial_term.astype(jnp.bfloat16)).astype(jnp.float32)
    partial_score = jnp.sum(flat_saved.astype(jnp.float32) * rounded_term, axis=1)
    moved_scores = lax.all_to_all(
        partial_score.reshape(local_experts, group_count, capacity),
        "grp",
        split_axis=1,
        concat_axis=1,
        tiled=True,
    )
    returned = lax.psum(moved_scores, "ep")
    summed = lax.psum_scatter(
        partial_term.astype(jnp.bfloat16), "ep", scatter_dimension=0, tiled=True
    ).astype(jnp.float32)
    own_prob = lax.dynamic_slice_in_dim(flat_prob, owner_index * share_rows, share_rows, 0)
    hidden_grad = (own_prob[:, None] * summed).astype(jnp.bfloat16)[None]
    pair_score = jnp.sum(
        jnp.where(slot_match, returned.reshape(slot_count, 1), 0.0), axis=0
    ).reshape(group_rows, top_count)
    weighted_mean = jnp.sum(route_probs * pair_score, axis=1, keepdims=True) / route_scale
    logit_terms = route_probs * (1.0 - chosen) * (pair_score - weighted_mean)
    router_grad = jnp.sum(jnp.where(picked, logit_terms[:, :, None], 0.0), axis=1).astype(
        jnp.bfloat16
    )
    input_grad = jnp.dot(router_grad, router_weight, preferred_element_type=jnp.float32).astype(
        jnp.bfloat16
    )
    return (weight_grad, hidden_grad, input_grad)


MESH = pl.DeviceIdType.MESH


def flip(a, j):
    out, bit = a, 1
    while bit <= j:
        if j & bit:
            out = out + bit * (1 - 2 * (a // bit % 2))
        bit *= 2
    return out


def fused_kernel(
    ids_hbm, logits_hbm, grad_hbm, rw_hbm, w_hbm, saved_hbm,
    weight_ref, hidden_ref, input_ref,
    ids_ref, logits_ref, rw_ref, w_ref, saved_ref, rows_all, notes_own, notes_all,
    spread_ref, saved_tok, scaled, part, recv_a, send_b, recv_b,
    score_own, score_recv, score_rows,
    in_sem, w_sem, rows_send, rows_recv, note_send, note_recv,
    a_send, a_recv, kept_recv, b_send, b_recv, sc_send, sc_recv,
):
    groups = lax.axis_size("grp")
    parts = lax.axis_size("ep")
    chips = parts // 2
    g = lax.axis_index("grp")
    k = lax.axis_index("ep")
    chip, core = k // 2, k % 2
    experts, rows = logits_ref.shape
    top = ids_ref.shape[0]
    _, local, _, width = part.shape
    features = rows_all.shape[1]
    half_groups = groups // 2
    half_tokens = half_groups * rows
    tokens = groups * rows
    span = saved_ref.shape[0] // local
    share = span // 2
    capacity = span // groups
    f32, bf16 = jnp.float32, jnp.bfloat16
    column, side = g // 2, lax.rem(g, 2)
    mate = g + 1 - 2 * side
    hops = list(range(half_groups - 1, 0, -1))
    turn = (((1,), (1,)), ((), ()))

    def iota(shape, dim):
        return lax.broadcasted_iota(jnp.int32, shape, dim)

    def mark(mask):
        return mask.astype(f32).astype(bf16)

    def dot(a, b):
        return jnp.dot(a, b, preferred_element_type=f32)

    barrier = pltpu.get_barrier_semaphore()
    peers = [(lax.rem(g + j, groups), k) for j in range(1, groups)]
    peers += [(g, lax.rem(k + j, parts)) for j in range(1, parts)]
    for peer in peers:
        pl.semaphore_signal(barrier, inc=1, device_id=peer, device_id_type=MESH)

    def block(b):
        return rows_all.at[pl.ds(pl.multiple_of(b * rows, rows), rows), :]

    fetch = [
        pltpu.make_async_copy(src, dst, in_sem.at[i])
        for i, (src, dst) in enumerate([
            (grad_hbm, block(g)), (logits_hbm, logits_ref), (ids_hbm, ids_ref),
            (saved_hbm, saved_ref), (rw_hbm, rw_ref),
        ])
    ]
    w_copy = pltpu.make_async_copy(w_hbm, w_ref, w_sem)
    for copy in [*fetch[1:3], fetch[0], w_copy, *fetch[3:]]:
        copy.start()

    def remote(src, dst, send, recv, to):
        return pltpu.make_async_remote_copy(
            src_ref=src, dst_ref=dst, send_sem=send, recv_sem=recv, device_id=to,
            device_id_type=MESH,
        )

    def rows_copy(b, to):
        return remote(block(b), block(b), rows_send, rows_recv.at[b], (to, k))

    def note_copy(b, to):
        return remote(notes_own.at[to], notes_all.at[b], note_send, note_recv, (to, k))

    fetch[1].wait()
    fetch[2].wait()
    sig = 1.0 / (1.0 + jnp.exp(-logits_ref[...]))
    ids = ids_ref[...]
    expert_iota = iota((experts, rows), 0)
    named = ids[0:1, :] == expert_iota
    for i in range(1, top):
        named = named | (ids[i : i + 1, :] == expert_iota)
    probs = route_scale * sig / jnp.sum(jnp.where(named, sig, 0.0), axis=0, keepdims=True)
    probs = jnp.where(named, probs, 0.0)
    rank = dot(mark(named), mark(iota((rows, rows), 0) < iota((rows, rows), 1)))
    base = (lax.rem(g, half_groups) * capacity).astype(f32)
    slots = jnp.where(named, base + rank, -1.0)
    kinds = 2 * local
    lanes = kinds * rows
    facts = jnp.concatenate([probs.astype(bf16), slots.astype(bf16)], axis=0)
    wide = dot(facts, mark(iota((rows, lanes), 1) % rows == iota((rows, lanes), 0)))
    line = iota((2 * experts, lanes), 0)
    kind = line // experts * local + line % local
    wide = jnp.where(kind == iota((2 * experts, lanes), 1) // rows, wide, 0.0).astype(bf16)
    owner = iota((groups, 2 * experts), 1) % experts // local
    notes = dot(mark(owner == iota((groups, 2 * experts), 0)), wide)
    for o in range(groups):
        notes_own[o] = notes[o : o + 1, :]
    pltpu.make_async_copy(notes_own.at[g], notes_all.at[g], note_recv).start()
    fetch[0].wait()
    pl.semaphore_wait(barrier, len(peers))
    for j in range(1, groups):
        note_copy(g, lax.rem(g + j, groups)).start()
    rows_copy(g, mate).start()
    for j in hops:
        rows_copy(g, flip(column, j) * 2 + side).start()

    order = [lax.rem(chip + 1 + i, chips) for i in range(chips)]
    partner = k + 1 - 2 * core

    def a_copy(b, i):
        if i == chips - 1:
            recv = kept_recv
        else:
            recv = a_recv.at[i, lax.rem(b, half_groups)]
        l = order[i]
        return remote(part.at[b, l], recv_a.at[b, l], a_send, recv, (g, partner))

    def multiply(*blocks):
        found = [block(b)[...] for b in blocks]
        found = found[0] if len(found) == 1 else jnp.concatenate(found, axis=0)
        for l in range(local):
            value = dot(found, w_ref[l]).astype(bf16)
            for i, b in enumerate(blocks):
                part[b, l] = value[i * rows : (i + 1) * rows]
        for i in range(chips):
            for b in blocks:
                pl.when(b // half_groups != core)(a_copy(b, i).start)

    def finish(b):
        at = lax.rem(b, half_groups)

        @pl.when(b // half_groups == core)
        def _():
            for i in range(chips - 1):
                l = order[i]
                a_copy(b, i).wait_recv()
                both = part[b, l].astype(f32) + recv_a[b, l].astype(f32)
                send_b[i, at] = both.astype(bf16)
                to = (g, l * 2 + core)
                remote(send_b.at[i, at], recv_b.at[chips - 2 - i, at], b_send, b_recv, to).start()

    eye = iota((rows, half_tokens), 0) == iota((rows, half_tokens), 1)

    slot = k * groups + g

    def score(b, home=False):
        for l in range(local):
            at = pl.ds(pl.multiple_of(b * rows, rows), rows)
            value = jnp.sum(
                saved_tok[l, at, :].astype(f32) * part[b, l].astype(f32), axis=1, keepdims=True
            )
            score_own[b, l : l + 1, :] = jnp.sum(
                jnp.where(eye, value, 0.0), axis=0, keepdims=True
            )
        if home:
            pltpu.make_async_copy(score_own.at[b], score_recv.at[slot], sc_recv).start()
        for dk in range(1 if home else 0, parts):
            to = (b, lax.rem(k + dk, parts))
            remote(score_own.at[b], score_recv.at[slot], sc_send, sc_recv, to).start()

    def tables():
        remote(notes_all, notes_all, note_send, note_recv, (g, k)).wait_recv()
        fetch[3].wait()
        diagonal = iota((rows, lanes), 1) % rows == iota((rows, lanes), 0)
        stack = [
            jnp.where(diagonal, jnp.broadcast_to(notes_all[b], (rows, lanes)), 0.0)
            for b in range(groups)
        ]
        stack = jnp.concatenate(stack, axis=0).astype(bf16)
        shape = (lanes, kinds * share)
        cols = dot(stack, mark(iota(shape, 0) // rows == iota(shape, 1) // share))
        spot = iota((tokens, share), 1).astype(f32)
        for l in range(local):
            weight = cols[:, l * share : (l + 1) * share]
            place = cols[:, (local + l) * share : (local + l + 1) * share]
            hit = place == spot
            match = mark(hit)
            scaled[l] = weight[:, 0:128]
            weight = jnp.where(hit, weight, 0.0).astype(bf16)
            for h in range(2):
                at = slice(h * half_tokens, (h + 1) * half_tokens)
                spread_ref[l, h] = weight[at]
                start = l * span + h * share
                saved_tok[l, at, :] = dot(
                    match[at], saved_ref[start : start + share, :]
                ).astype(bf16)

    near = [flip(column, j) * 2 + side for j in hops]
    far = [flip(column, j) * 2 + 1 - side for j in hops]
    w_copy.wait()
    multiply(g)
    rows_copy(mate, g).wait_recv()
    rows_copy(mate, near[-1]).start()
    multiply(mate)
    finish(g)
    tables()
    score(g, home=True)
    score(mate)
    for i, b in enumerate(near):
        rows_copy(b, g).wait_recv()
        if i < len(near) - 1:
            rows_copy(b, mate).start()
    multiply(*near)
    finish(mate)
    for b in near:
        score(b)
    for b in near:
        finish(b)
    last = None
    for b in [far[-1], *far[:-1]]:
        rows_copy(b, g).wait_recv()
        multiply(b)
        if last is not None:
            finish(last)
        score(b)
        last = b

    step = min(width, 256)

    def weigh(l):
        weighed = jnp.concatenate(
            [
                (scaled[l] * rows_all[:, n : n + 128].astype(f32)).astype(bf16)
                for n in range(0, features, 128)
            ],
            axis=1,
        )
        for n in range(0, width, step):
            weight_ref[l, :, n : n + step] = lax.dot_general(
                weighed, saved_tok[l, :, n : n + step], (((0,), (0,)), ((), ())),
                preferred_element_type=f32,
            ).astype(bf16)

    weigh(0)
    finish(last)
    for l in range(1, local):
        weigh(l)
    unit = mark(iota((share, share), 0) == iota((share, share), 1))
    spread = lax.dot_general(
        unit, spread_ref[chip, core], turn, preferred_element_type=f32
    ).astype(bf16)
    total = None
    held = pl.ds(core * half_groups, half_groups)
    whole = part.at[0:half_groups, 0]
    remote(whole, whole, a_send, kept_recv, (g, partner)).wait_recv()
    total = part[held, chip].astype(f32) + recv_a[held, chip].astype(f32)
    if chips > 1:
        arrived = recv_b.at[0 : chips - 1]
        remote(arrived, arrived, b_send, b_recv, (g, partner)).wait_recv()
    for i in range(chips - 1):
        total = total + recv_b[i].astype(f32)
    hidden_ref[...] = dot(spread, total.reshape(half_tokens, width).astype(bf16)).astype(bf16)

    remote(score_recv, score_recv, sc_send, sc_recv, (g, partner)).wait_recv()
    for o in range(groups):
        value = score_recv[o]
        for y in range(1, parts):
            value = value + score_recv[y * groups + o]
        score_rows[o * local : (o + 1) * local, :] = value
    pair = score_rows[:, 0:rows]
    mean = jnp.sum(probs * pair, axis=0, keepdims=True) / route_scale
    terms = jnp.where(named, probs * (1.0 - sig) * (pair - mean), 0.0).astype(bf16)
    turned = lax.dot_general(
        mark(iota((rows, rows), 0) == iota((rows, rows), 1)), terms, turn,
        preferred_element_type=f32,
    ).astype(bf16)
    fetch[4].wait()
    input_ref[...] = dot(turned, rw_ref[...]).astype(bf16)

    def sent(ref, sem):
        remote(ref, ref, sem, kept_recv, (g, partner)).wait_send()

    sent(rows_all.at[0 : (groups - 1) * rows, :], rows_send)
    sent(notes_all.at[0 : groups - 1], note_send)
    sent(part.at[0:half_groups], a_send)
    sent(send_b, b_send)
    sent(score_recv.at[0 : parts * groups - 1], sc_send)


def write_kernel(weight_ref, hidden_ref, input_ref, weight_hbm, hidden_hbm, input_hbm, sem):
    copies = [
        pltpu.make_async_copy(hidden_ref, hidden_hbm, sem.at[0]),
        pltpu.make_async_copy(input_ref, input_hbm, sem.at[1]),
    ]
    local, features, _ = weight_ref.shape
    cut = features // 4
    for l in range(local):
        for n in range(4):
            at = pl.ds(n * cut, cut)
            copies.append(
                pltpu.make_async_copy(
                    weight_ref.at[l, at, :], weight_hbm.at[l, at, :], sem.at[2 + l * 4 + n]
                )
            )
    for copy in copies:
        copy.start()
    for copy in copies:
        copy.wait()


def fused(out_grad, expert_ids, router_logits, router_weight, expert_weight, hidden_saved):
    groups, parts = lax.axis_size("grp"), lax.axis_size("ep")
    rows, features = out_grad.shape
    experts = router_logits.shape[1]
    top = expert_ids.shape[1]
    local, _, width = expert_weight.shape
    slots = hidden_saved.shape[1]
    span = slots // local
    half_groups = groups // 2
    half_tokens = half_groups * rows
    tokens = groups * rows
    share = span // 2
    chips = parts // 2
    f32, bf16 = jnp.float32, jnp.bfloat16
    vmem = pl.BlockSpec(memory_space=pltpu.VMEM)
    hbm = pl.BlockSpec(memory_space=pltpu.HBM)
    anyspace = pl.BlockSpec(memory_space=pl.ANY)
    dma = pltpu.SemaphoreType.DMA
    out_shape = (
        jax.ShapeDtypeStruct((local, features, width), bf16),
        jax.ShapeDtypeStruct((share, width), bf16),
        jax.ShapeDtypeStruct((rows, features), bf16),
    )
    pin = pltpu.with_memory_space_constraint
    outs = pl.pallas_call(
        fused_kernel,
        out_shape=tuple(pltpu.VMEM(x.shape, x.dtype) for x in out_shape),
        in_specs=[hbm] * 6,
        out_specs=(vmem, vmem, vmem),
        scratch_shapes=[
            pltpu.VMEM((top, rows), jnp.int32),
            pltpu.VMEM((experts, rows), f32),
            pltpu.VMEM((experts, features), bf16),
            pltpu.VMEM((local, features, width), bf16),
            pltpu.VMEM((slots, width), bf16),
            pltpu.VMEM((tokens, features), bf16),
            pltpu.VMEM((groups, 1, 2 * local * rows), f32),
            pltpu.VMEM((groups, 1, 2 * local * rows), f32),
            pltpu.VMEM((local, 2, half_tokens, share), bf16),
            pltpu.VMEM((local, tokens, width), bf16),
            pltpu.VMEM((local, tokens, 128), f32),
            pltpu.VMEM((groups, local, rows, width), bf16),
            pltpu.VMEM((groups, local, rows, width), bf16),
            pltpu.VMEM((chips - 1, half_groups, rows, width), bf16),
            pltpu.VMEM((chips - 1, half_groups, rows, width), bf16),
            pltpu.VMEM((groups, local, half_tokens), f32),
            pltpu.VMEM((parts * groups, local, half_tokens), f32),
            pltpu.VMEM((experts, half_tokens), f32),
            dma((5,)), dma, dma, dma((groups,)), dma, dma,
            dma, dma((chips - 1, half_groups)), dma, dma, dma, dma, dma,
        ],
        compiler_params=pltpu.CompilerParams(
            collective_id=0, has_side_effects=True, vmem_limit_bytes=40 * 1024 * 1024
        ),
    )(*[
        pin(x, pltpu.HBM)
        for x in (
            expert_ids.T, router_logits.T, out_grad, router_weight, expert_weight,
            hidden_saved.reshape(slots, width),
        )
    ])
    weight_grad, hidden, input_grad = pl.pallas_call(
        write_kernel,
        out_shape=out_shape,
        in_specs=[anyspace] * 3,
        out_specs=[hbm] * 3,
        scratch_shapes=[dma((2 + 4 * local,))],
        compiler_params=pltpu.CompilerParams(vmem_limit_bytes=16 * 1024 * 1024),
    )(*[pin(x, pltpu.VMEM) for x in outs])
    return weight_grad, hidden[None], input_grad


def choose(*args):
    out_grad, _, _, _, expert_weight, hidden_saved = args
    groups, parts = lax.axis_size("grp"), lax.axis_size("ep")
    rows, local = out_grad.shape[0], expert_weight.shape[0]
    slots_for_one = hidden_saved.shape[1] // groups
    lanes = groups // 2 * rows
    capacity = slots_for_one // local
    share = groups // 2 * capacity
    fits = rows <= capacity and lanes % 128 == 0 and share % 128 == 0 and share <= 256
    fits = fits and 2 * local * rows % 128 == 0 and groups & (groups - 1) == 0
    if parts == 2 * local and parts > 2 and groups % 2 == 0 and fits:
        return fused(*args)
    return body(*args)


def solution(mesh):
    in_specs = (
        P("grp", "ep"),
        P("grp", None),
        P("grp", None),
        P(None, "ep"),
        P("grp", "ep", None),
        P("grp", None, None),
    )
    out_specs = (P("grp", "ep", None), P("grp", "ep", None), P("grp", "ep"))
    return jax.shard_map(choose, mesh=mesh, in_specs=in_specs, out_specs=out_specs, check_vma=False)
```

time: 28.3 us -> 25.3 us (0.89)
  Pallas kernels: 27.5 us -> 24.5 us
    pallas_call x1, Pallas kernels: 25.3 us -> 22.3 us  [fused(): pl.pallas_call(fused_kernel, out_shape=tuple((pltpu.VMEM(x.shape, x.dtype...]
where the time goes in v4:
time: 25.3 us; the launch traced here: 25.1 us
  Pallas kernels  24.5 us (97%)
  between operations  0.64 us (3%)
    pallas_call x1, Pallas kernels, fused(): pl.pallas_call(fused_kernel, out_shape=tuple((pltpu.VMEM(x.shape, x.dtype...  22.3 us
    pallas_call x1, Pallas kernels, fused(): pl.pallas_call(write_kernel, out_shape=out_shape, in_specs=[anyspace] * 3...  2.2 us

profile of v4, /device:TPU:0, one launch (start us, length us, event | category | flops | bytes accessed | tf_op | source)
XLA Modules:
  0.0 25.1 jit_solution(11707770967238202265)
XLA Ops:
  0.6 22.3 %shard_map.85 = (bf16[2,1024,1024]{2,1,0:T(8,128)(2,1)S(1)}, bf16[128,1024]{1,0:T(8,128)(2,1)S(1)}, bf16[32,1024]{1,0:T(8,128)(2,1)S(1)}) custom-call(s32[8,32]{1,0:T(8,128)} %bitcast.6, f32[16,32]{1,0:T(8,128)} %bitcast.5, bf16[32,1024]{1,0:T(8,128)(2,1)} %grad_hbm.1, bf16[16,1024]{1,0:T(8,128)(2,1)} %rw_hbm.1, bf16[2,1024,1024]{2,1,0:T(8,128)(2,1)} %w_hbm.1, ...), custom_call_target="tpu_custom_call" | custom-call | tf_op jit(solution)/shard_map/pallas_call | solution.py:436
  22.9 2.2 %shard_map.86 = (bf16[2,1024,1024]{2,1,0:T(8,128)(2,1)}, bf16[128,1024]{1,0:T(8,128)(2,1)}, bf16[32,1024]{1,0:T(8,128)(2,1)}) custom-call(bf16[2,1024,1024]{2,1,0:T(8,128)(2,1)S(1)} %get-tuple-element.9.weight_ref, bf16[128,1024]{1,0:T(8,128)(2,1)S(1)} %get-tuple-element.10.hidden_ref, bf16[32,1024]{1,0:T(8,128)(2,1)S(1)} %get-tuple-element.11.input_ref), custom_call_target="tpu_custom_call" | custom-call | tf_op jit(solution)/shard_map/pallas_call | solution.py:473

commit v5 on v4

--- a/solution.py
+++ b/solution.py
@@ -112,10 +112,10 @@
 
 def fused_kernel(
     ids_hbm, logits_hbm, grad_hbm, rw_hbm, w_hbm, saved_hbm,
-    weight_ref, hidden_ref, input_ref,
-    ids_ref, logits_ref, rw_ref, w_ref, saved_ref, rows_all, notes_own, notes_all,
+    weight_ref, total_out, spread_out, score_out, prob_out, gain_out, rw_ref,
+    ids_ref, logits_ref, w_ref, saved_ref, rows_all, notes_own, notes_all,
     spread_ref, saved_tok, scaled, part, recv_a, send_b, recv_b,
-    score_own, score_recv, score_rows,
+    score_own, score_recv,
     in_sem, w_sem, rows_send, rows_recv, note_send, note_recv,
     a_send, a_recv, kept_recv, b_send, b_recv, sc_send, sc_recv,
 ):
@@ -177,7 +177,8 @@
         )
 
     def rows_copy(b, to):
-        return remote(block(b), block(b), rows_send, rows_recv.at[b], (to, k))
+        data = block(b)
+        return remote(data, data, rows_send, rows_recv.at[b], (to, k))
 
     def note_copy(b, to):
         return remote(notes_own.at[to], notes_all.at[b], note_send, note_recv, (to, k))
@@ -211,9 +212,11 @@
     pl.semaphore_wait(barrier, len(peers))
     for j in range(1, groups):
         note_copy(g, lax.rem(g + j, groups)).start()
+    near = [flip(column, j) * 2 + side for j in hops]
+    far = [flip(column, j) * 2 + 1 - side for j in hops]
     rows_copy(g, mate).start()
-    for j in hops:
-        rows_copy(g, flip(column, j) * 2 + side).start()
+    for j, b in zip(hops, near):
+        rows_copy(g, b).start()
 
     order = [lax.rem(chip + 1 + i, chips) for i in range(chips)]
     partner = k + 1 - 2 * core
@@ -296,35 +299,40 @@
                     match[at], saved_ref[start : start + share, :]
                 ).astype(bf16)
 
-    near = [flip(column, j) * 2 + side for j in hops]
-    far = [flip(column, j) * 2 + 1 - side for j in hops]
     w_copy.wait()
     multiply(g)
     rows_copy(mate, g).wait_recv()
     rows_copy(mate, near[-1]).start()
     multiply(mate)
     finish(g)
+    ahead = max(len(near) - 2, 0)
     tables()
     score(g, home=True)
     score(mate)
-    for i, b in enumerate(near):
+    finish(mate)
+    for j, b in zip(hops, near):
         rows_copy(b, g).wait_recv()
-        if i < len(near) - 1:
+        if j > 1:
             rows_copy(b, mate).start()
     multiply(*near)
-    finish(mate)
     for b in near:
+        score(b)
+    first = [far[-1], *far[:ahead]]
+    for b in first:
+        rows_copy(b, g).wait_recv()
+    multiply(*first)
+    for b in first:
         score(b)
     for b in near:
         finish(b)
-    last = None
-    for b in [far[-1], *far[:-1]]:
+    last = far[ahead:-1]
+    for b in last:
         rows_copy(b, g).wait_recv()
         multiply(b)
-        if last is not None:
-            finish(last)
+    for b in last:
         score(b)
-        last = b
+    for b in first:
+        finish(b)
 
     step = min(width, 256)
 
@@ -343,14 +351,17 @@
             ).astype(bf16)
 
     weigh(0)
-    finish(last)
+    for b in last:
+        finish(b)
     for l in range(1, local):
         weigh(l)
     unit = mark(iota((share, share), 0) == iota((share, share), 1))
-    spread = lax.dot_general(
+    spread_out[...] = lax.dot_general(
         unit, spread_ref[chip, core], turn, preferred_element_type=f32
     ).astype(bf16)
-    total = None
+    prob_out[...] = probs
+    gain_out[...] = jnp.where(named, probs * (1.0 - sig), 0.0)
+    fetch[4].wait()
     held = pl.ds(core * half_groups, half_groups)
     whole = part.at[0:half_groups, 0]
     remote(whole, whole, a_send, kept_recv, (g, partner)).wait_recv()
@@ -360,23 +371,13 @@
         remote(arrived, arrived, b_send, b_recv, (g, partner)).wait_recv()
     for i in range(chips - 1):
         total = total + recv_b[i].astype(f32)
-    hidden_ref[...] = dot(spread, total.reshape(half_tokens, width).astype(bf16)).astype(bf16)
-
+    total_out[...] = total.reshape(half_tokens, width).astype(bf16)
     remote(score_recv, score_recv, sc_send, sc_recv, (g, partner)).wait_recv()
     for o in range(groups):
         value = score_recv[o]
         for y in range(1, parts):
             value = value + score_recv[y * groups + o]
-        score_rows[o * local : (o + 1) * local, :] = value
-    pair = score_rows[:, 0:rows]
-    mean = jnp.sum(probs * pair, axis=0, keepdims=True) / route_scale
-    terms = jnp.where(named, probs * (1.0 - sig) * (pair - mean), 0.0).astype(bf16)
-    turned = lax.dot_general(
-        mark(iota((rows, rows), 0) == iota((rows, rows), 1)), terms, turn,
-        preferred_element_type=f32,
-    ).astype(bf16)
-    fetch[4].wait()
-    input_ref[...] = dot(turned, rw_ref[...]).astype(bf16)
+        score_out[o * local : (o + 1) * local, :] = value
 
     def sent(ref, sem):
         remote(ref, ref, sem, kept_recv, (g, partner)).wait_send()
@@ -388,23 +389,37 @@
     sent(score_recv.at[0 : parts * groups - 1], sc_send)
 
 
-def write_kernel(weight_ref, hidden_ref, input_ref, weight_hbm, hidden_hbm, input_hbm, sem):
+def write_kernel(
+    weight_ref, total_ref, spread_ref, score_ref, prob_ref, gain_ref, rw_ref,
+    weight_hbm, hidden_hbm, input_hbm, hidden_ref, input_ref, sem,
+):
+    local = weight_ref.shape[0]
+    rows = input_ref.shape[0]
+    f32, bf16 = jnp.float32, jnp.bfloat16
     copies = [
-        pltpu.make_async_copy(hidden_ref, hidden_hbm, sem.at[0]),
-        pltpu.make_async_copy(input_ref, input_hbm, sem.at[1]),
+        pltpu.make_async_copy(weight_ref.at[l], weight_hbm.at[l], sem.at[2 + l])
+        for l in range(local)
     ]
-    local, features, _ = weight_ref.shape
-    cut = features // 4
-    for l in range(local):
-        for n in range(4):
-            at = pl.ds(n * cut, cut)
-            copies.append(
-                pltpu.make_async_copy(
-                    weight_ref.at[l, at, :], weight_hbm.at[l, at, :], sem.at[2 + l * 4 + n]
-                )
-            )
     for copy in copies:
         copy.start()
+    hidden_ref[...] = jnp.dot(
+        spread_ref[...], total_ref[...], preferred_element_type=f32
+    ).astype(bf16)
+    copies.append(pltpu.make_async_copy(hidden_ref, hidden_hbm, sem.at[0]))
+    copies[-1].start()
+    pair = score_ref[:, 0:rows]
+    mean = jnp.sum(prob_ref[...] * pair, axis=0, keepdims=True) / route_scale
+    terms = (gain_ref[...] * (pair - mean)).astype(bf16)
+    eye = lax.broadcasted_iota(jnp.int32, (rows, rows), 0) == lax.broadcasted_iota(
+        jnp.int32, (rows, rows), 1
+    )
+    turned = lax.dot_general(
+        eye.astype(f32).astype(bf16), terms, (((1,), (1,)), ((), ())),
+        preferred_element_type=f32,
+    ).astype(bf16)
+    input_ref[...] = jnp.dot(turned, rw_ref[...], preferred_element_type=f32).astype(bf16)
+    copies.append(pltpu.make_async_copy(input_ref, input_hbm, sem.at[1]))
+    copies[-1].start()
     for copy in copies:
         copy.wait()
 
@@ -435,13 +450,20 @@
     pin = pltpu.with_memory_space_constraint
     outs = pl.pallas_call(
         fused_kernel,
-        out_shape=tuple(pltpu.VMEM(x.shape, x.dtype) for x in out_shape),
+        out_shape=(
+            pltpu.VMEM((local, features, width), bf16),
+            pltpu.VMEM((share, width), bf16),
+            pltpu.VMEM((share, half_tokens), bf16),
+            pltpu.VMEM((experts, half_tokens), f32),
+            pltpu.VMEM((experts, rows), f32),
+            pltpu.VMEM((experts, rows), f32),
+            pltpu.VMEM((experts, features), bf16),
+        ),
         in_specs=[hbm] * 6,
-        out_specs=(vmem, vmem, vmem),
+        out_specs=(vmem,) * 7,
         scratch_shapes=[
             pltpu.VMEM((top, rows), jnp.int32),
             pltpu.VMEM((experts, rows), f32),
-            pltpu.VMEM((experts, features), bf16),
             pltpu.VMEM((local, features, width), bf16),
             pltpu.VMEM((slots, width), bf16),
             pltpu.VMEM((tokens, features), bf16),
@@ -456,7 +478,6 @@
             pltpu.VMEM((chips - 1, half_groups, rows, width), bf16),
             pltpu.VMEM((groups, local, half_tokens), f32),
             pltpu.VMEM((parts * groups, local, half_tokens), f32),
-            pltpu.VMEM((experts, half_tokens), f32),
             dma((5,)), dma, dma, dma((groups,)), dma, dma,
             dma, dma((chips - 1, half_groups)), dma, dma, dma, dma, dma,
         ],
@@ -473,9 +494,12 @@
     weight_grad, hidden, input_grad = pl.pallas_call(
         write_kernel,
         out_shape=out_shape,
-        in_specs=[anyspace] * 3,
+        in_specs=[anyspace, *[vmem] * 6],
         out_specs=[hbm] * 3,
-        scratch_shapes=[dma((2 + 4 * local,))],
+        scratch_shapes=[
+            pltpu.VMEM((share, width), bf16), pltpu.VMEM((rows, features), bf16),
+            dma((2 + local,)),
+        ],
         compiler_params=pltpu.CompilerParams(vmem_limit_bytes=16 * 1024 * 1024),
     )(*[pin(x, pltpu.VMEM) for x in outs])
     return weight_grad, hidden[None], input_grad
@@ -491,7 +515,7 @@
     share = groups // 2 * capacity
     fits = rows <= capacity and lanes % 128 == 0 and share % 128 == 0 and share <= 256
     fits = fits and 2 * local * rows % 128 == 0 and groups & (groups - 1) == 0
-    if parts == 2 * local and parts > 2 and groups % 2 == 0 and fits:
+    if parts == 2 * local and parts > 2 and groups > 2 and fits:
         return fused(*args)
     return body(*args)
 

time: 25.3 us -> 25.2 us (level)
  no operation moved by 1% of the time
where the time goes in v5:
time: 25.2 us; the launch traced here: 25 us
  Pallas kernels  24.3 us (96%)
  between operations  0.64 us (3%)
    pallas_call x1, Pallas kernels, fused(): pl.pallas_call(fused_kernel, out_shape=(pltpu.VMEM((local, features, widt...  22.2 us
    pallas_call x1, Pallas kernels, fused(): pl.pallas_call(write_kernel, out_shape=out_shape, in_specs=[anyspace, *[v...  2.15 us

profile of v5, /device:TPU:0, one launch (start us, length us, event | category | flops | bytes accessed | tf_op | source)
XLA Modules:
  0.0 25.0 jit_solution(16011089107664327245)
XLA Ops:
  0.6 22.2 %shard_map.85 = (bf16[2,1024,1024]{2,1,0:T(8,128)(2,1)S(1)}, bf16[128,1024]{1,0:T(8,128)(2,1)S(1)}, bf16[128,128]{1,0:T(8,128)(2,1)S(1)}, f32[16,128]{1,0:T(8,12...) custom-call(s32[8,32]{1,0:T(8,128)} %bitcast.6, f32[16,32]{1,0:T(8,128)} %bitcast.5, ...), custom_call_target="tpu_custom_call" | custom-call | tf_op jit(solution)/shard_map/pallas_call | solution.py:451
  22.8 2.1 %shard_map.86 = (bf16[2,1024,1024]{2,1,0:T(8,128)(2,1)}, bf16[128,1024]{1,0:T(8,128)(2,1)}, bf16[32,1024]{1,0:T(8,128)(2,1)}) custom-call(bf16[2,1024,1024]{2,1,0:T(8,128)(2,1)S(1)} %get-tuple-element.13.weight_ref, bf16[128,1024]{1,0:T(8,128)(2,1)S(1)} %get-tuple-element.14.total_ref, bf16[128,128]{1,0:T(8,128)(2,1)S(1)} %get-tuple-element.15.spread_ref, ...), custom_call_target="tpu_custom_call" | custom-call | tf_op jit(solution)/shard_map/pallas_call | solution.py:494
